TPU v7x, 16 devices: a whole 2x2x2 slice. The times are simulated.
16 devices in a mesh: replica: 2 (over z), fsdp: 8 (over y, x, core).
Axes of the slice: x: 2, y: 2, z: 2, core: 2. Of those that a mesh axis runs over, the one named last changes fastest.
Arguments:
- block_in: bfloat16 [1, 32768, 2048], P(None, ('replica', 'fsdp'))
- grad_out: bfloat16 [32768, 2048], P(('replica', 'fsdp'))
- w_up: bfloat16 [1, 2048, 5632], P(None, 'fsdp')
- w_lin: bfloat16 [1, 2048, 5632], P(None, 'fsdp')
- w_down: bfloat16 [1, 5632, 2048], P(None, 'fsdp')
Outputs:
- output 1: float32 [1, 2048, 5632], P(None, 'fsdp')
- output 2: float32 [1, 2048, 5632], P(None, 'fsdp')
- output 3: float32 [1, 5632, 2048], P(None, 'fsdp')
- output 4: bfloat16 [32768, 2048], P(('replica', 'fsdp'))
All inputs are finite; a program needn't handle non-finite values.
Results may differ from a plain program's by a relative error of at most 0.001.
Values are sent between devices in bfloat16 or wider.
A program may use at most 1 GiB of HBM per device.

v0:
```python
import jax
import jax.numpy as jnp
from jax import lax
from jax.sharding import PartitionSpec as P

NORM_EPS = 1e-5


def layer_grad(h_in, grad_acc, up_w, lin_w, down_w):
    h_f32 = h_in.astype(jnp.float32)
    inv_rms = lax.rsqrt(jnp.mean(h_f32 * h_f32, axis=-1, keepdims=True) + NORM_EPS)
    normed = h_f32 * inv_rms
    normed_b = normed.astype(jnp.bfloat16)
    pre_up = jnp.einsum('td,df->tf', normed_b, up_w, preferred_element_type=jnp.float32)
    pre_lin = jnp.einsum('td,df->tf', normed_b, lin_w, preferred_element_type=jnp.float32)
    up_sig = jax.nn.sigmoid(pre_up)
    up_act = pre_up * up_sig
    act_b = (up_act * pre_lin).astype(jnp.bfloat16)
    grad_b = grad_acc.astype(jnp.bfloat16)
    d_act = jnp.einsum('td,fd->tf', grad_b, down_w, preferred_element_type=jnp.float32)
    d_up = (d_act * pre_lin * up_sig * (1.0 + pre_up * (1.0 - up_sig))).astype(jnp.bfloat16)
    d_lin = (d_act * up_act).astype(jnp.bfloat16)
    g_down = jnp.einsum('tf,td->fd', act_b, grad_b, preferred_element_type=jnp.float32)
    g_up = jnp.einsum('td,tf->df', normed_b, d_up, preferred_element_type=jnp.float32)
    g_lin = jnp.einsum('td,tf->df', normed_b, d_lin, preferred_element_type=jnp.float32)
    d_norm = jnp.einsum('tf,df->td', d_up, up_w, preferred_element_type=jnp.float32) + jnp.einsum('tf,df->td', d_lin, lin_w, preferred_element_type=jnp.float32)
    d_h = inv_rms * (d_norm - normed * jnp.mean(d_norm * normed, axis=-1, keepdims=True))
    return grad_acc + d_h, g_up, g_lin, g_down


def reduce_shard(full_grad):
    own_rows = lax.psum_scatter(full_grad, 'fsdp', scatter_dimension=0, tiled=True)
    return lax.psum(own_rows, 'replica')


def solution(mesh):
    tok_spec = P(('replica', 'fsdp'), None)
    act_spec = P(None, ('replica', 'fsdp'), None)
    weight_spec = P(None, 'fsdp', None)

    def local_step(block_in, grad_out, w_up, w_lin, w_down):
        layers = block_in.shape[0]
        grad_acc = grad_out.astype(jnp.float32)
        up_list = []
        lin_list = []
        down_list = []
        for layer_idx in reversed(range(layers)):
            up_full = lax.all_gather(w_up[layer_idx], 'fsdp', axis=0, tiled=True)
            lin_full = lax.all_gather(w_lin[layer_idx], 'fsdp', axis=0, tiled=True)
            down_full = lax.all_gather(w_down[layer_idx], 'fsdp', axis=0, tiled=True)
            grad_acc, g_up, g_lin, g_down = layer_grad(block_in[layer_idx], grad_acc, up_full, lin_full, down_full)
            up_list.insert(0, reduce_shard(g_up))
            lin_list.insert(0, reduce_shard(g_lin))
            down_list.insert(0, reduce_shard(g_down))
        return jnp.stack(up_list), jnp.stack(lin_list), jnp.stack(down_list), grad_acc.astype(jnp.bfloat16)

    return jax.shard_map(local_step, mesh=mesh, in_specs=(act_spec, tok_spec, weight_spec, weight_spec, weight_spec), out_specs=(weight_spec, weight_spec, weight_spec, tok_spec), check_vma=False)
```

profile of v0, /device:TPU:0, one launch (start us, length us, event | category | flops | bytes accessed | tf_op | source)
XLA Modules:
  0.0 1687.0 jit_solution(8016848624059468828)
XLA Ops:
  7.9 0.7 all-gather.11.cloned.1.call-update
  9.4 12.2 copy.9
  21.7 5.1 fusion.20
  26.8 98.4 %all-gather.9.cloned.1.call-done = bf16[1,2048,5632]{2,1,0:T(8,128)(2,1)} async-done(((bf16[1,256,5632]{2,1,0:T(8,128)(2,1)}), bf16[1,2048,5632]{2,1,0:T(8,128)(2,1)}) %all-gather.9.cloned.1.call-update) | async-done | bytes 23068688 | tf_op jit(solution)/shard_map/all_gather | solution.py:49
  125.2 59.2 %fusion.8 = f32[2048,5632]{1,0:T(8,128)} fusion(bf16[1,2048,5632]{2,1,0:T(8,128)(2,1)} %all-gather.9.cloned.1.call-done, bf16[1,2048,2048]{1,2,0:T(8,128)(2,1)} %copy.9, f32[2048]{0:T(1024)S(1)} %add_rsqrt_fusion), kind=kOutput, calls=%fused_computation.12 | convolution fusion | flops 47257223168 | bytes 77602816 | tf_op jit(solution)/shard_map/td,df->tf/dot_general | solution.py:15
  184.5 55.2 %all-gather.11.cloned.1.call-done = bf16[1,2048,5632]{2,1,0:T(8,128)(2,1)} async-done(((bf16[1,256,5632]{2,1,0:T(8,128)(2,1)}), bf16[1,2048,5632]{2,1,0:T(8,128)(2,1)}) %all-gather.11.cloned.1.call-update) | async-done | bytes 23068688 | tf_op jit(solution)/shard_map/all_gather | solution.py:48
  239.7 59.5 %fusion.4 = f32[2048,5632]{1,0:T(8,128)} fusion(bf16[1,2048,5632]{2,1,0:T(8,128)(2,1)} %all-gather.11.cloned.1.call-done, bf16[1,2048,2048]{1,2,0:T(8,128)(2,1)} %copy.9, f32[2048]{0:T(1024)S(1)} %add_rsqrt_fusion), kind=kOutput, calls=%fused_computation.8 | convolution fusion | flops 47257223168 | bytes 77602816 | tf_op jit(solution)/shard_map/td,df->tf/dot_general | solution.py:14
  299.2 54.9 %all-gather.7.cloned.1.call-done = bf16[1,5632,2048]{2,1,0:T(8,128)(2,1)} async-done(((bf16[1,704,2048]{2,1,0:T(8,128)(2,1)}), bf16[1,5632,2048]{2,1,0:T(8,128)(2,1)}) %all-gather.7.cloned.1.call-update) | async-done | bytes 23068688 | tf_op jit(solution)/shard_map/all_gather | solution.py:50
  354.1 85.1 %multiply_convert_fusion.1 = (bf16[2048,5632]{1,0:T(8,128)(2,1)}, bf16[2048,5632]{1,0:T(8,128)(2,1)}) fusion(f32[2048,5632]{1,0:T(8,128)} %fusion.4, f32[2048,5632]{1,0:T(8,128)} %fusion.8, bf16[2048,2048]{1,0:T(8,128)(2,1)} %param.6, bf16[1,5632,2048]{2,1,0:T(8,128)(2,1)} %all-gather.7.cloned.1.call-done), kind=kOutput, calls=%fused_computation.1 | convolution fusion | flops 47394586624 | bytes 169869312 | tf_op jit(solution)/shard_map/td,fd->tf/dot_general | solution.py:20
  439.2 58.3 %fusion.25 = f32[2048,5632]{1,0:T(8,128)} fusion(bf16[2048,5632]{1,0:T(8,128)(2,1)} %get-tuple-element.11, bf16[1,2048,2048]{1,2,0:T(8,128)(2,1)} %copy.9, f32[2048]{0:T(1024)S(1)} %add_rsqrt_fusion), kind=kOutput, calls=%fused_computation.28 | convolution fusion | flops 47257223168 | bytes 77602816 | tf_op jit(solution)/shard_map/td,tf->df/dot_general | solution.py:25
  497.6 58.4 %fusion.27 = f32[2048,5632]{1,0:T(8,128)} fusion(bf16[2048,5632]{1,0:T(8,128)(2,1)} %get-tuple-element.12, bf16[1,2048,2048]{1,2,0:T(8,128)(2,1)} %copy.9, f32[2048]{0:T(1024)S(1)} %add_rsqrt_fusion), kind=kOutput, calls=%fused_computation.29 | convolution fusion | flops 47257223168 | bytes 77602816 | tf_op jit(solution)/shard_map/td,tf->df/dot_general | solution.py:24
  556.1 61.2 %fusion.1 = f32[5632,2048]{1,0:T(8,128)} fusion(bf16[2048,2048]{1,0:T(8,128)(2,1)} %param.6, f32[2048,5632]{1,0:T(8,128)} %fusion.8, f32[2048,5632]{1,0:T(8,128)} %fusion.4), kind=kOutput, calls=%fused_computation.5 | convolution fusion | flops 47313846272 | bytes 146800640 | tf_op jit(solution)/shard_map/tf,td->fd/dot_general | solution.py:23
  617.4 12.5 copy.10
  629.9 125.6 %reduce-scatter.6.cloned.1.call-done = f32[256,5632]{1,0:T(8,128)} async-done(((f32[2048,5632]{1,0:T(8,128)}), f32[256,5632]{1,0:T(8,128)}) %reduce-scatter.6.cloned.1.call-update) | async-done | bytes 5767184 | tf_op jit(solution)/shard_map/reduce_scatter | solution.py:32
  755.5 261.3 %reduce-scatter.4.cloned.1.call-done = f32[256,5632]{1,0:T(8,128)} async-done(((f32[2048,5632]{1,0:T(8,128)}), f32[256,5632]{1,0:T(8,128)}) %reduce-scatter.4.cloned.1.call-update) | async-done | bytes 5767184 | tf_op jit(solution)/shard_map/reduce_scatter | solution.py:32
  1016.8 261.3 %reduce-scatter.8.cloned.1.call-done = f32[704,2048]{1,0:T(8,128)} async-done(((f32[5632,2048]{1,0:T(8,128)}), f32[704,2048]{1,0:T(8,128)}) %reduce-scatter.8.cloned.1.call-update) | async-done | bytes 5767184 | tf_op jit(solution)/shard_map/reduce_scatter | solution.py:32
  1278.2 59.5 %fusion.2 = f32[2048,2048]{0,1:T(8,128)} fusion(bf16[2048,5632]{1,0:T(8,128)(2,1)} %get-tuple-element.12, bf16[1,2048,5632]{2,1,0:T(8,128)(2,1)} %all-gather.11.cloned.1.call-done), kind=kOutput, calls=%fused_computation.6 | convolution fusion | flops 47244640256 | bytes 62914560 | tf_op jit(solution)/shard_map/tf,df->td/dot_general | solution.py:26
  1337.7 60.6 %fusion.15 = (f32[2048]{0:T(1024)S(1)}, f32[2048,2048]{0,1:T(8,128)}) fusion(bf16[1,2048,2048]{1,2,0:T(8,128)(2,1)} %copy.9, f32[2048]{0:T(1024)S(1)} %copy-done.2, f32[2048,2048]{0,1:T(8,128)} %fusion.2, bf16[2048,5632]{1,0:T(8,128)(2,1)} %get-tuple-element.11, bf16[1,2048,5632]{2,1,0:T(8,128)(2,1)} %all-gather.9.cloned.1.call-done), kind=kOutput, calls=%fused_computation.21 | convolution fusion | flops 47265611776 | bytes 88096768 | tf_op jit(solution)/shard_map/tf,df->td/dot_general | solution.py:26
  1398.3 13.1 fusion.19
  1411.4 12.2 copy.11
  1423.7 242.5 %all-reduce.3.cloned.1.call-done = (f32[1,256,5632]{2,1,0:T(8,128)}, f32[1,256,5632]{2,1,0:T(8,128)}, f32[1,704,2048]{2,1,0:T(8,128)}) async-done(((f32[1,256,5632]{2,1,0:T(8,128)}, f32[1,256,5632]{2,1,0:T(8,128)}, f32[1,704,2048]{2,1,0:T(8,128)}), (f32[1,256,5632]{2,1,0:T(8,128)}, f32[1,256,5632]{2,1,0:T(8,128)}, f32[1,704,2048]{2,1,0:T(8,128)})) %all-reduce.3.cloned.1.call-update) | async-done | bytes 17301520 | tf_op jit(solution)/shard_map/psum | solution.py:33
  1666.1 5.7 copy.15
  1671.8 5.6 copy.16
  1677.4 2.5 copy.17
  (26 shorter events, 1.7 us)
Async XLA Ops:
  7.2 118.1 %all-gather.9.cloned.1.call-start = ((), (), s32[]{:S(2)}) async-start(), calls=%async_computation.7 | async-start | bytes 25952256 | tf_op jit(solution)/shard_map/all_gather | solution.py:49
  7.9 231.8 %all-gather.11.cloned.1.call-start = ((), (), s32[]{:S(2)}) async-start(), calls=%async_computation.8 | async-start | bytes 25952256 | tf_op jit(solution)/shard_map/all_gather | solution.py:48
  8.6 345.4 %all-gather.7.cloned.1.call-start = ((), (), s32[]{:S(2)}) async-start(), calls=%async_computation.6 | async-start | bytes 25952256 | tf_op jit(solution)/shard_map/all_gather | solution.py:50
  9.4 746.2 %reduce-scatter.6.cloned.1.call-start = ((), (), s32[]{:S(2)}) async-start(), calls=%async_computation.4 | async-start | bytes 51904512 | tf_op jit(solution)/shard_map/reduce_scatter | solution.py:32
  26.8 470.8 %copy-start.1 = (f32[2048]{0:T(1024)}, f32[2048]{0:T(1024)S(1)}, u32[]{:S(2)}) copy-start(f32[2048]{0:T(1024)S(1)} %add_rsqrt_fusion) | copy-start | bytes 24580
  497.6 519.3 %reduce-scatter.4.cloned.1.call-start = ((), (), s32[]{:S(2)}) async-start(), calls=%async_computation.3 | async-start | bytes 51904512 | tf_op jit(solution)/shard_map/reduce_scatter | solution.py:32
  556.1 722.1 %reduce-scatter.8.cloned.1.call-start = ((), (), s32[]{:S(2)}) async-start(), calls=%async_computation.5 | async-start | bytes 51904512 | tf_op jit(solution)/shard_map/reduce_scatter | solution.py:32
  617.3 1048.8 %all-reduce.3.cloned.1.call-start = ((), (), s32[]{:S(2)}) async-start(), calls=%async_computation.9 | async-start | bytes 34603008 | tf_op jit(solution)/shard_map/psum | solution.py:33
  1278.1 59.5 %copy-start.2 = (f32[2048]{0:T(1024)S(1)}, f32[2048]{0:T(1024)}, u32[]{:S(2)}) copy-start(f32[2048]{0:T(1024)} %copy-done.1) | copy-start | bytes 24580
  1337.7 60.6 %copy-start = (bf16[1,2048,2048]{1,2,0:T(8,128)(2,1)S(1)}, bf16[1,2048,2048]{1,2,0:T(8,128)(2,1)}, u32[]{:S(2)}) copy-start(bf16[1,2048,2048]{1,2,0:T(8,128)(2,1)} %copy.9) | copy-start | bytes 25165828
  1666.1 11.3 slice-start
  1666.1 11.3 slice-start.1
Sparse Core Ops, SparseCore 0:
  9.8 115.3 all-gather.8
  127.1 112.5 all-gather.10
  241.5 112.5 all-gather.6
  497.7 257.8 reduce-scatter.5
  759.0 257.8 reduce-scatter.3
  1020.3 257.8 reduce-scatter.7
  1280.8 385.2 all-reduce.2
where the time goes:
time: 1690 us
  waiting for transfers between devices  1100 us (65%)
  matrix products  502 us (30%)
  local copies, waits for them, and re-layouts  50.8 us (3%)
  other arithmetic  18.3 us (1%)
    reduce_scatter x3, waiting for transfers between devices, reduce_shard(): lax.psum_scatter(full_grad, 'fsdp', scatter_dimension=0, tiled=True)  648 us
    psum x1, waiting for transfers between devices, reduce_shard(): return lax.psum(own_rows, 'replica')  242 us
    all_gather x1, waiting for transfers between devices, local_step(): lin_full = lax.all_gather(w_lin[layer_idx], 'fsdp', axis=0, tiled=True)  98.4 us
    dot_general x1, matrix products, layer_grad(): jnp.einsum('td,fd->tf', grad_b, down_w, preferred_element_type=jnp.float32)  85.1 us
    dot_general x1, matrix products, layer_grad(): jnp.einsum('tf,td->fd', act_b, grad_b, preferred_element_type=jnp.float32)  61.2 us
    dot_general x1, matrix products, layer_grad(): jnp.einsum('tf,df->td', d_lin, lin_w, preferred_element_type=jnp.float32)  60.6 us
    dot_general x1, matrix products, layer_grad(): jnp.einsum('tf,df->td', d_up, up_w, preferred_element_type=jnp.float32)  59.5 us
    dot_general x1, matrix products, layer_grad(): jnp.einsum('td,df->tf', normed_b, up_w, preferred_element_type=jnp.float32)  59.5 us
  transfers between devices with their start and end apart: 7, of which 7 were waited for; matrix products, arithmetic and copies ran while one was open for 25% of the time, Pallas kernels for 0%

commit v1 on v0

v1 whole, which is shorter than its diff:
```python
import jax
import jax.numpy as jnp
from jax import lax
from jax.sharding import PartitionSpec as P


NORM_EPS = 1e-5
F32 = jnp.float32
BF16 = jnp.bfloat16


def dot(a, b, da, db):
    return lax.dot_general(a, b, (((da,), (db,)), ((), ())), preferred_element_type=F32)


def after(value, *others):
    return lax.optimization_barrier((value, others))[0]


def pick(arr, idx, axis):
    return lax.dynamic_index_in_dim(arr, idx, axis, keepdims=False)


def solution(mesh):
    n_fsdp = mesh.shape['fsdp']
    tok_spec = P(('replica', 'fsdp'), None)
    act_spec = P(None, ('replica', 'fsdp'), None)
    weight_spec = P(None, 'fsdp', None)

    def swap(value, bit):
        return lax.ppermute(value, 'fsdp', [(i, i ^ bit) for i in range(n_fsdp)])

    def swap_z(value):
        return lax.ppermute(value, 'replica', [(0, 1), (1, 0)])

    def split_parity(w, blk):
        cols = [w[:, i * blk:(i + 1) * blk] for i in range(n_fsdp)]
        return jnp.concatenate(cols[0::2] + cols[1::2], axis=1)

    def local_step(block_in, grad_out, w_up, w_lin, w_down):
        layers, tok, dim = block_in.shape
        ff = w_up.shape[2]
        half = ff // 2
        rows = dim // n_fsdp
        ff_blk = ff // n_fsdp
        fi = lax.axis_index('fsdp').astype(jnp.uint32)
        core = (fi & 1).astype(jnp.int32)
        pos = (((fi >> 1) & 1).astype(jnp.int32), (fi >> 2).astype(jnp.int32))

        def slab1(g, first):
            g = g.reshape((2, 2) + g.shape[1:])
            return pick(g, 1 - pos[first], 1 - first)

        def send1(slab, first):
            return swap(slab, 2 << first)

        def add1(g, got, first):
            g = g.reshape((2, 2) + g.shape[1:])
            return pick(g, pos[first], 1 - first) + got

        def send2(part, first):
            return swap(pick(part, 1 - pos[1 - first], 0), 4 >> first)

        def add2(part, got, first):
            return pick(part, pos[1 - first], 0) + got

        def place_cols(totals):
            out = []
            for tot in totals:
                mine = lax.dynamic_slice_in_dim(tot, core * rows, rows, axis=0)
                other = lax.dynamic_slice_in_dim(tot, (1 - core) * rows, rows, axis=0)
                got = swap(other, 1)
                even = jnp.where(core == 0, mine, got)
                odd = jnp.where(core == 0, got, mine)
                for j in range(tot.shape[1] // ff_blk):
                    out += [even[:, j * ff_blk:(j + 1) * ff_blk], odd[:, j * ff_blk:(j + 1) * ff_blk]]
            return jnp.concatenate(out, axis=1)

        def take_cols(full):
            return lax.dynamic_slice_in_dim(full, core * half, half, axis=1)

        grad_acc = grad_out.astype(F32)
        up_list = []
        lin_list = []
        down_list = []
        for l in reversed(range(layers)):
            up_eo = split_parity(w_up[l], ff_blk)
            lin_eo = split_parity(after(w_lin[l], up_eo), ff_blk)
            lin_w = take_cols(lax.all_gather(lin_eo, 'fsdp', axis=0, tiled=True))
            up_w = take_cols(lax.all_gather(up_eo, 'fsdp', axis=0, tiled=True))
            down_w = lax.all_gather(after(w_down[l], lin_eo), 'fsdp', axis=0, tiled=True)
            down_w = pick(down_w.reshape(n_fsdp // 2, 2, ff_blk, dim), core, 1).reshape(half, dim)
            h_f32 = block_in[l].astype(F32)
            inv_rms = lax.rsqrt(jnp.mean(h_f32 * h_f32, axis=-1, keepdims=True) + NORM_EPS)
            normed = h_f32 * inv_rms
            n_own = normed.astype(BF16)
            gb_own = grad_acc.astype(BF16)
            n = jnp.concatenate([n_own, swap(n_own, 1)], axis=0)
            gb = jnp.concatenate([gb_own, swap(gb_own, 1)], axis=0)

            pre_lin = dot(n, lin_w, 1, 0)
            pre_up = dot(n, up_w, 1, 0)
            up_sig = jax.nn.sigmoid(pre_up)
            act_b = (pre_up * up_sig * pre_lin).astype(BF16)
            act_b, pre_up, pre_lin = lax.optimization_barrier((act_b, pre_up, pre_lin))

            hd = dim // 2
            down = [dot(act_b, gb[:, j * hd:(j + 1) * hd], 0, 0).reshape(4, ff_blk, hd) for j in range(2)]
            down_slab = [slab1(g, j) for j, g in enumerate(down)]
            down_got = [send1(g, j) for j, g in enumerate(down_slab)]

            up_sig = jax.nn.sigmoid(pre_up)
            up_act = pre_up * up_sig
            d_act = dot(after(gb, down_slab), down_w, 1, 1)
            d_up = (d_act * pre_lin * up_sig * (1.0 + pre_up * (1.0 - up_sig))).astype(BF16)
            d_lin = (d_act * up_act).astype(BF16)

            hc = half // 2
            up = [dot(n, d_up[:, j * hc:(j + 1) * hc], 0, 0).reshape(4, 2 * rows, hc) for j in range(2)]
            down_got = after(down_got, *up)
            down_part = [add1(down[j], down_got[j], j) for j in range(2)]
            down_got = [send2(down_part[j], j) for j in range(2)]
            up = after(up, down_part)
            up_slab = [slab1(up[j], j) for j in range(2)]
            up_got = [send1(up_slab[j], j) for j in range(2)]

            n_late, d_lin_late = after((n, d_lin), up_slab)
            lin = [dot(n_late, d_lin_late[:, j * hc:(j + 1) * hc], 0, 0).reshape(4, 2 * rows, hc) for j in range(2)]
            down_got = after(down_got, *lin)
            down_own = [add2(down_part[j], down_got[j], j) for j in range(2)]
            down_z = [swap_z(v) for v in down_own]

            d_up_late, d_lin_late = after((d_up, d_lin), down_own)
            d_norm_par = dot(d_up_late[tok:], up_w, 1, 1) + dot(d_lin_late[tok:], lin_w, 1, 1)
            d_norm_got = swap(d_norm_par, 1)
            up_got = after(up_got, d_norm_par)
            up_part = [add1(up[j], up_got[j], j) for j in range(2)]
            up_got = [send2(up_part[j], j) for j in range(2)]
            lin = after(lin, up_part)
            lin_slab = [slab1(lin[j], j) for j in range(2)]
            lin_got = [send1(lin_slab[j], j) for j in range(2)]

            d_up_late, d_lin_late = after((d_up_late, d_lin_late), lin_slab)
            d_norm = dot(d_up_late[:tok], up_w, 1, 1) + dot(d_lin_late[:tok], lin_w, 1, 1) + d_norm_got
            d_h = inv_rms * (d_norm - normed * jnp.mean(d_norm * normed, axis=-1, keepdims=True))
            grad_acc = grad_acc + d_h

            up_got = after(up_got, grad_acc)
            up_own = [add2(up_part[j], up_got[j], j) for j in range(2)]
            up_z = [swap_z(v) for v in up_own]
            lin_got, down_z = after((lin_got, down_z), up_own)
            down_list.insert(0, jnp.concatenate([a + b for a, b in zip(down_own, down_z)], axis=1))
            lin_part = [add1(lin[j], lin_got[j], j) for j in range(2)]
            lin_got = [send2(lin_part[j], j) for j in range(2)]
            up_z = after(up_z, lin_part)
            up_list.insert(0, place_cols([a + b for a, b in zip(up_own, up_z)]))
            lin_own = [add2(lin_part[j], lin_got[j], j) for j in range(2)]
            lin_list.insert(0, place_cols([v + swap_z(v) for v in lin_own]))
        return jnp.stack(up_list), jnp.stack(lin_list), jnp.stack(down_list), grad_acc.astype(BF16)

    return jax.shard_map(local_step, mesh=mesh, in_specs=(act_spec, tok_spec, weight_spec, weight_spec, weight_spec), out_specs=(weight_spec, weight_spec, weight_spec, tok_spec), check_vma=False)
```

time: 1690 us -> 1430 us (0.85)
  waiting for transfers between devices: 1100 us -> 591 us
  other arithmetic: 18.3 us -> 126 us
  local copies, waits for them, and re-layouts: 50.8 us -> 128 us
  matrix products: 502 us -> 541 us
  starting transfers between devices: 0.28 us -> 20.8 us
    reduce_scatter x3 -> x0, waiting for transfers between devices: 648 us -> none  [reduce_shard(): lax.psum_scatter(full_grad, 'fsdp', scatter_dimension=0, tiled=True)]
    ppermute x0 -> x25, waiting for transfers between devices: none -> 482 us  [the longest x19 298 us: swap(): return lax.ppermute(value, 'fsdp', [(i, i ^ bit) for i in range(n_fsdp)])]
    psum x1 -> x0, waiting for transfers between devices: 242 us -> none  [reduce_shard(): return lax.psum(own_rows, 'replica')]
    all_gather x3, waiting for transfers between devices: 209 us -> 109 us  [the longest x1 56.1 us: local_step(): lin_w = take_cols(lax.all_gather(lin_eo, 'fsdp', axis=0, tiled=True))]
    add x0 -> x19, other arithmetic: none -> 87.4 us  [the longest x6 30.3 us: add1(): return pick(g, pos[first], 1 - first) + got]
    squeeze x0 -> x12, local copies, waits for them, and re-layouts: none -> 42.8 us  [pick(): return lax.dynamic_index_in_dim(arr, idx, axis, keepdims=False)]
    dot_general x8 -> x13, matrix products: 502 us -> 541 us  [dot(): lax.dot_general(a, b, (((da,), (db,)), ((), ())), preferred_element_type=...]
    concatenate x0 -> x5, local copies, waits for them, and re-layouts: none -> 36.8 us  [the longest x2 14.9 us: place_cols(): return jnp.concatenate(out, axis=1)]
  transfers between devices with their start and end apart: 7 -> 28, of which waited for: 7 -> 12; matrix products, arithmetic and copies ran while one was open for 25% -> 46% of each run, Pallas kernels for 0% -> 0%
where the time goes in v1:
time: 1430 us; the launch traced here: 1420 us
  waiting for transfers between devices  591 us (41%)
  matrix products  541 us (38%)
  local copies, waits for them, and re-layouts  128 us (9%)
  other arithmetic  126 us (9%)
  starting transfers between devices  20.8 us (1%)
  between operations  14.3 us (1%)
    dot_general x13, matrix products, dot(): lax.dot_general(a, b, (((da,), (db,)), ((), ())), preferred_element_type=...  541 us
    ppermute x19, waiting for transfers between devices, swap(): return lax.ppermute(value, 'fsdp', [(i, i ^ bit) for i in range(n_fsdp)])  298 us
    ppermute x6, waiting for transfers between devices, swap_z(): return lax.ppermute(value, 'replica', [(0, 1), (1, 0)])  184 us
    all_gather x1, waiting for transfers between devices, local_step(): lin_w = take_cols(lax.all_gather(lin_eo, 'fsdp', axis=0, tiled=True))  56.1 us
    all_gather x1, waiting for transfers between devices, local_step(): up_w = take_cols(lax.all_gather(up_eo, 'fsdp', axis=0, tiled=True))  53.3 us
    squeeze x12, local copies, waits for them, and re-layouts, pick(): return lax.dynamic_index_in_dim(arr, idx, axis, keepdims=False)  42.8 us
    add x6, other arithmetic, add1(): return pick(g, pos[first], 1 - first) + got  30.3 us
  transfers between devices with their start and end apart: 28, of which 12 were waited for; matrix products, arithmetic and copies ran while one was open for 46% of the time, Pallas kernels for 0%

profile of v1, /device:TPU:0, one launch (start us, length us, event | category | flops | bytes accessed | tf_op | source)
XLA Modules:
  0.0 1421.0 jit_solution(7468050146236537271)
XLA Ops:
  54.8 15.1 %pad_maximum_fusion = bf16[4096,2048]{1,0:T(8,128)(2,1)} fusion(bf16[2048,2048]{1,0:T(8,128)(2,1)} %collective-permute-done, bf16[2048,2048]{1,0:T(8,128)(2,1)} %fusion.2), kind=kLoop, calls=%fused_computation.14 | loop fusion | flops 33554432 | bytes 33554432 | tf_op jit(solution)/shard_map/concatenate | solution.py:98
  79.7 53.3 %all-gather.4.cloned.1.call-done = bf16[2048,5632]{1,0:T(8,128)(2,1)} async-done(((bf16[256,5632]{1,0:T(8,128)(2,1)}), bf16[2048,5632]{1,0:T(8,128)(2,1)}) %all-gather.4.cloned.1.call-update) | async-done | bytes 23068688 | tf_op jit(solution)/shard_map/all_gather | solution.py:90
  133.1 58.9 %fusion.35 = f32[4096,2816]{1,0:T(8,128)} fusion(bf16[2048,5632]{1,0:T(8,128)(2,1)} %all-gather.4.cloned.1.call-done, s32[]{:T(128)S(6)} %select_n.95, bf16[2048,2048]{1,0:T(8,128)(2,1)} %collective-permute-done, bf16[2048,2048]{1,0:T(8,128)(2,1)} %fusion.2), kind=kOutput, calls=%fused_computation.39 | convolution fusion | flops 47278194688 | bytes 74448896 | tf_op jit(solution)/shard_map/dot_general | solution.py:13
  192.0 56.1 %all-gather.6.cloned.1.call-done = bf16[2048,5632]{1,0:T(8,128)(2,1)} async-done(((bf16[256,5632]{1,0:T(8,128)(2,1)}), bf16[2048,5632]{1,0:T(8,128)(2,1)}) %all-gather.6.cloned.1.call-update) | async-done | bytes 23068688 | tf_op jit(solution)/shard_map/all_gather | solution.py:89
  248.1 63.9 %multiply_convert_fusion.2 = (bf16[4096,2816]{1,0:T(8,128)(2,1)}, f32[4096,2816]{1,0:T(8,128)}) fusion(f32[4096,2816]{1,0:T(8,128)} %fusion.35, bf16[2048,5632]{1,0:T(8,128)(2,1)} %all-gather.6.cloned.1.call-done, s32[]{:T(128)S(6)} %select_n.95, bf16[2048,2048]{1,0:T(8,128)(2,1)} %collective-permute-done, bf16[2048,2048]{1,0:T(8,128)(2,1)} %fusion.2), kind=kOutput, calls=%fused_computation.3 | convolution fusion | flops 47347400704 | bytes 143654912 | tf_op jit(solution)/shard_map/dot_general | solution.py:13
  312.0 34.0 %fusion.37 = f32[2816,1024]{1,0:T(8,128)} fusion(bf16[4096,2816]{1,0:T(8,128)(2,1)} %get-tuple-element.35, bf16[4096,2048]{1,0:T(8,128)(2,1)} %constant_dynamic-update-slice_fusion), kind=kOutput, calls=%fused_computation.41 | convolution fusion | flops 23622320128 | bytes 42991616 | tf_op jit(solution)/shard_map/dot_general | solution.py:13
  352.6 33.8 %fusion.39 = f32[2816,1024]{1,0:T(8,128)} fusion(bf16[4096,2816]{1,0:T(8,128)(2,1)} %get-tuple-element.35, bf16[4096,2048]{1,0:T(8,128)(2,1)} %constant_dynamic-update-slice_fusion), kind=kOutput, calls=%fused_computation.43 | convolution fusion | flops 23622320128 | bytes 42991616 | tf_op jit(solution)/shard_map/dot_general | solution.py:13
  404.0 79.4 %multiply_convert_fusion = (bf16[4096,2816]{1,0:T(8,128)(2,1)}, bf16[4096,2816]{1,0:T(8,128)(2,1)}) fusion(f32[4096,2816]{1,0:T(8,128)} %fusion.35, f32[4096,2816]{1,0:T(8,128)} %get-tuple-element.38, bf16[4096,2048]{1,0:T(8,128)(2,1)} %constant_dynamic-update-slice_fusion, bf16[2816,2048]{1,0:T(8,128)(2,1)} %bitcast.91), kind=kOutput, calls=%fused_computation | convolution fusion | flops 47394586624 | bytes 166723584 | tf_op jit(solution)/shard_map/dot_general | solution.py:13
  483.4 34.2 %fusion.8 = f32[2048,1408]{1,0:T(8,128)} fusion(bf16[4096,2816]{1,0:T(8,128)(2,1)} %get-tuple-element.54, bf16[2048,2048]{1,0:T(8,128)(2,1)} %collective-permute-done, bf16[2048,2048]{1,0:T(8,128)(2,1)} %fusion.2), kind=kOutput, calls=%fused_computation.16 | convolution fusion | flops 23655874560 | bytes 39845888 | tf_op jit(solution)/shard_map/dot_general | solution.py:13
  517.7 34.1 %fusion.10 = f32[2048,1408]{1,0:T(8,128)} fusion(bf16[4096,2816]{1,0:T(8,128)(2,1)} %get-tuple-element.54, bf16[2048,2048]{1,0:T(8,128)(2,1)} %collective-permute-done, bf16[2048,2048]{1,0:T(8,128)(2,1)S(1)} %copy-done), kind=kOutput, calls=%fused_computation.18 | convolution fusion | flops 23655874560 | bytes 39845888 | tf_op jit(solution)/shard_map/dot_general | solution.py:13
  577.1 34.3 %fusion.20 = f32[2048,1408]{1,0:T(8,128)} fusion(bf16[4096,2048]{1,0:T(8,128)(2,1)} %pad_maximum_fusion, bf16[4096,2816]{1,0:T(8,128)(2,1)} %get-tuple-element.55), kind=kOutput, calls=%fused_computation.28 | convolution fusion | flops 23622320128 | bytes 39845888 | tf_op jit(solution)/shard_map/dot_general | solution.py:13
  611.4 34.1 %fusion.22 = f32[2048,1408]{1,0:T(8,128)} fusion(bf16[4096,2048]{1,0:T(8,128)(2,1)} %pad_maximum_fusion, bf16[4096,2816]{1,0:T(8,128)(2,1)} %get-tuple-element.55), kind=kOutput, calls=%fused_computation.30 | convolution fusion | flops 23622320128 | bytes 39845888 | tf_op jit(solution)/shard_map/dot_general | solution.py:13
  653.5 32.4 %fusion.16 = f32[2048,2048]{1,0:T(8,128)} fusion(bf16[4096,2816]{1,0:T(8,128)(2,1)} %get-tuple-element.55, bf16[2048,5632]{1,0:T(8,128)(2,1)} %all-gather.6.cloned.1.call-done, s32[]{:T(128)S(6)} %select_n.95), kind=kOutput, calls=%fused_computation.24 | convolution fusion | flops 23622320128 | bytes 39845892 | tf_op jit(solution)/shard_map/dot_general | solution.py:13
  686.0 33.4 %fusion.26 = f32[2048,2048]{1,0:T(8,128)} fusion(f32[2048,2048]{1,0:T(8,128)} %fusion.16, bf16[4096,2816]{1,0:T(8,128)(2,1)} %get-tuple-element.54, bf16[2048,5632]{1,0:T(8,128)(2,1)} %all-gather.4.cloned.1.call-done, s32[]{:T(128)S(6)} %select_n.95), kind=kOutput, calls=%fused_computation.32 | convolution fusion | flops 23626514432 | bytes 56623108 | tf_op jit(solution)/shard_map/dot_general | solution.py:13
  722.9 123.5 %collective-permute-done.5 = f32[2,512,1408]{2,1,0:T(8,128)S(1)} collective-permute-done((f32[2,512,1408]{2,1,0:T(8,128)}, f32[2,512,1408]{2,1,0:T(8,128)S(1)}, u32[]{:S(2)}, u32[]{:S(2)}) %collective-permute-start.5) | collective-permute-done | bytes 5767200 | tf_op jit(solution)/shard_map/ppermute | solution.py:31
  876.0 32.0 %fusion.12 = f32[2048,2048]{1,0:T(8,128)} fusion(bf16[4096,2816]{1,0:T(8,128)(2,1)} %get-tuple-element.55, bf16[2048,5632]{1,0:T(8,128)(2,1)} %all-gather.6.cloned.1.call-done, s32[]{:T(128)S(6)} %select_n.95), kind=kOutput, calls=%fused_computation.20 | convolution fusion | flops 23622320128 | bytes 39845892 | tf_op jit(solution)/shard_map/dot_general | solution.py:13
  908.4 35.8 %fusion.3 = (f32[2048]{0:T(1024)S(1)}, f32[2048,2048]{1,0:T(8,128)}) fusion(bf16[1,2048,2048]{2,1,0:T(8,128)(2,1)} %param.5, f32[2048]{0:T(1024)S(1)} %copy-done.17, f32[2048,2048]{1,0:T(8,128)} %collective-permute-done.10, f32[2048,2048]{1,0:T(8,128)} %fusion.12, bf16[2048,5632]{1,0:T(8,128)(2,1)} %all-gather.4.cloned.1.call-done, s32[]{:T(128)S(6)} %select_n.95, ...), kind=kOutput, calls=%fused_computation.9 | convolution fusion | flops 23647483904 | bytes 81805312 | tf_op jit(solution)/shard_map/dot_general | solution.py:13
  944.2 113.5 %collective-permute-done.9 = f32[512,1408]{1,0:T(8,128)} collective-permute-done((f32[512,1408]{1,0:T(8,128)}, f32[512,1408]{1,0:T(8,128)}, u32[]{:S(2)}, u32[]{:S(2)}) %collective-permute-start.9) | collective-permute-done | bytes 2883616 | tf_op jit(solution)/shard_map/ppermute | solution.py:31
  1059.0 16.1 %fusion.6 = bf16[2048,2048]{1,0:T(8,128)(2,1)} fusion(f32[2048,2048]{1,0:T(8,128)} %get-tuple-element.109, bf16[2048,2048]{1,0:T(8,128)(2,1)} %param.6, bf16[1,2048,2048]{2,1,0:T(8,128)(2,1)} %param.5, f32[2048]{0:T(1024)S(1)} %broadcast_multiply_fusion, f32[2048]{0:T(1024)S(1)} %copy-done.17), kind=kLoop, calls=%fused_computation.12 | loop fusion | flops 33554432 | bytes 41959424 | tf_op jit(solution)/shard_map/add | solution.py:146
  1082.8 37.5 %collective-permute-done.15 = f32[704,1024]{1,0:T(8,128)S(1)} collective-permute-done((f32[704,1024]{1,0:T(8,128)S(1)}, f32[704,1024]{1,0:T(8,128)S(1)}, u32[]{:S(2)}, u32[]{:S(2)}) %collective-permute-start.15) | collective-permute-done | bytes 2883616 | tf_op jit(solution)/shard_map/ppermute | solution.py:34
  1140.1 48.6 %collective-permute-done.22 = f32[512,1408]{1,0:T(8,128)S(1)} collective-permute-done((f32[512,1408]{1,0:T(8,128)S(1)}, f32[512,1408]{1,0:T(8,128)S(1)}, u32[]{:S(2)}, u32[]{:S(2)}) %collective-permute-start.22) | collective-permute-done | bytes 2883616 | tf_op jit(solution)/shard_map/ppermute | solution.py:31
  1206.9 58.7 %collective-permute-done.12 = f32[512,1408]{1,0:T(8,128)} collective-permute-done((f32[512,1408]{1,0:T(8,128)}, f32[512,1408]{1,0:T(8,128)}, u32[]{:S(2)}, u32[]{:S(2)}) %collective-permute-start.12) | collective-permute-done | bytes 2883616 | tf_op jit(solution)/shard_map/ppermute | solution.py:34
  1286.4 40.9 %collective-permute-done.23 = f32[512,1408]{1,0:T(8,128)} collective-permute-done((f32[512,1408]{1,0:T(8,128)}, f32[512,1408]{1,0:T(8,128)}, u32[]{:S(2)}, u32[]{:S(2)}) %collective-permute-start.23) | collective-permute-done | bytes 2883616 | tf_op jit(solution)/shard_map/ppermute | solution.py:34
  1338.2 46.8 %collective-permute-done.20 = f32[512,1408]{1,0:T(8,128)} collective-permute-done((f32[512,1408]{1,0:T(8,128)}, f32[512,1408]{1,0:T(8,128)}, u32[]{:S(2)}, u32[]{:S(2)}) %collective-permute-start.20) | collective-permute-done | bytes 2883616 | tf_op jit(solution)/shard_map/ppermute | solution.py:34
  (143 shorter events, 256.2 us)
Async XLA Ops:
  7.2 125.9 %all-gather.4.cloned.1.call-start = ((), (), s32[]{:S(2)}) async-start(), calls=%async_computation | async-start | bytes 25952256 | tf_op jit(solution)/shard_map/all_gather | solution.py:90
  17.5 230.6 %all-gather.6.cloned.1.call-start = ((), (), s32[]{:S(2)}) async-start(), calls=%async_computation.1 | async-start | bytes 25952256 | tf_op jit(solution)/shard_map/all_gather | solution.py:89
  25.8 368.1 %all-gather.8.cloned.1.call-start = ((), (), s32[]{:S(2)}) async-start(), calls=%async_computation.2 | async-start | bytes 25952256 | tf_op jit(solution)/shard_map/all_gather | solution.py:91
  352.2 199.6 %collective-permute-start.3 = (f32[2,704,1024]{2,1,0:T(8,128)}, f32[2,704,1024]{2,1,0:T(8,128)}, u32[]{:S(2)}, u32[]{:S(2)}) collective-permute-start(f32[2,704,1024]{2,1,0:T(8,128)} %dynamic-slice_bitcast_fusion.4), channel_id=1, source_target_pairs={{0,4},{1,5},{2,6},{3,7},{4,0},{5,1},{6,2},{7,3},{8,12},{9,13},{10,... | collective-permute-start | bytes 17301512 | tf_op jit(solution)/shard_map/ppermute | solution.py:31
  392.5 159.3 %collective-permute-start.2 = (f32[2,704,1024]{2,1,0:T(8,128)}, f32[2,704,1024]{2,1,0:T(8,128)}, u32[]{:S(2)}, u32[]{:S(2)}) collective-permute-start(f32[2,704,1024]{2,1,0:T(8,128)} %dynamic-slice_bitcast_fusion.5), channel_id=1, source_target_pairs={{0,2},{1,3},{2,0},{3,1},{4,6},{5,7},{6,4},{7,5},{8,10},{9,11},{10,... | collective-permute-start | bytes 17301512 | tf_op jit(solution)/shard_map/ppermute | solution.py:31
  575.0 70.6 %collective-permute-start.7 = (f32[704,1024]{1,0:T(8,128)S(1)}, f32[704,1024]{1,0:T(8,128)}, u32[]{:S(2)}, u32[]{:S(2)}) collective-permute-start(f32[704,1024]{1,0:T(8,128)S(1)} %dynamic-slice_bitcast_fusion.10), channel_id=1, source_target_pairs={{0,2},{1,3},{2,0},{3,1},{4,6},{5,7},{6,4},{7,5},{8,10},{9,11},{10,... | collective-permute-start | bytes 8650760 | tf_op jit(solution)/shard_map/ppermute | solution.py:31
  575.5 70.0 %collective-permute-start.6 = (f32[704,1024]{1,0:T(8,128)S(1)}, f32[704,1024]{1,0:T(8,128)}, u32[]{:S(2)}, u32[]{:S(2)}) collective-permute-start(f32[704,1024]{1,0:T(8,128)S(1)} %dynamic-slice_bitcast_fusion.11), channel_id=1, source_target_pairs={{0,4},{1,5},{2,6},{3,7},{4,0},{5,1},{6,2},{7,3},{8,12},{9,13},{10,... | collective-permute-start | bytes 8650760 | tf_op jit(solution)/shard_map/ppermute | solution.py:31
  719.4 188.6 %collective-permute-start.10 = (f32[2048,2048]{1,0:T(8,128)}, f32[2048,2048]{1,0:T(8,128)}, u32[]{:S(2)}, u32[]{:S(2)}) collective-permute-start(f32[2048,2048]{1,0:T(8,128)} %fusion.26), channel_id=1, source_target_pairs={{0,1},{1,0},{2,3},{3,2},{4,5},{5,4},{6,7},{7,6},{8,9},{9,8},{10,11... | collective-permute-start | bytes 50331656 | tf_op jit(solution)/shard_map/ppermute | solution.py:31
  719.5 126.9 %collective-permute-start.5 = (f32[2,512,1408]{2,1,0:T(8,128)}, f32[2,512,1408]{2,1,0:T(8,128)S(1)}, u32[]{:S(2)}, u32[]{:S(2)}) collective-permute-start(f32[2,512,1408]{2,1,0:T(8,128)} %dynamic-slice_bitcast_fusion.2), channel_id=1, source_target_pairs={{0,4},{1,5},{2,6},{3,7},{4,0},{5,1},{6,2},{7,3},{8,12},{9,13},{10,... | collective-permute-start | bytes 17301512 | tf_op jit(solution)/shard_map/ppermute | solution.py:31
  720.0 126.6 %collective-permute-start.4 = (f32[2,512,1408]{2,1,0:T(8,128)}, f32[2,512,1408]{2,1,0:T(8,128)S(1)}, u32[]{:S(2)}, u32[]{:S(2)}) collective-permute-start(f32[2,512,1408]{2,1,0:T(8,128)} %dynamic-slice_bitcast_fusion.3), channel_id=1, source_target_pairs={{0,2},{1,3},{2,0},{3,1},{4,6},{5,7},{6,4},{7,5},{8,10},{9,11},{10,... | collective-permute-start | bytes 17301512 | tf_op jit(solution)/shard_map/ppermute | solution.py:31
  721.4 361.4 %collective-permute-start.16 = (f32[704,1024]{1,0:T(8,128)}, f32[704,1024]{1,0:T(8,128)}, u32[]{:S(2)}, u32[]{:S(2)}) collective-permute-start(f32[704,1024]{1,0:T(8,128)} %bitcast_add_fusion.10), channel_id=1, source_target_pairs={{0,8},{8,0},{1,9},{9,1},{2,10},{10,2},{3,11},{11,3},{4,12},{12,4},... | collective-permute-start | bytes 8650760 | tf_op jit(solution)/shard_map/ppermute | solution.py:34
  863.2 257.0 %collective-permute-start.14 = (f32[2,512,1408]{2,1,0:T(8,128)}, f32[2,512,1408]{2,1,0:T(8,128)}, u32[]{:S(2)}, u32[]{:S(2)}) collective-permute-start(f32[2,512,1408]{2,1,0:T(8,128)} %dynamic-slice_bitcast_fusion), channel_id=1, source_target_pairs={{0,4},{1,5},{2,6},{3,7},{4,0},{5,1},{6,2},{7,3},{8,12},{9,13},{10,... | collective-permute-start | bytes 17301512 | tf_op jit(solution)/shard_map/ppermute | solution.py:31
  870.4 251.5 %collective-permute-start.13 = (f32[2,512,1408]{2,1,0:T(8,128)}, f32[2,512,1408]{2,1,0:T(8,128)}, u32[]{:S(2)}, u32[]{:S(2)}) collective-permute-start(f32[2,512,1408]{2,1,0:T(8,128)} %dynamic-slice_bitcast_fusion.1), channel_id=1, source_target_pairs={{0,2},{1,3},{2,0},{3,1},{4,6},{5,7},{6,4},{7,5},{8,10},{9,11},{10,... | collective-permute-start | bytes 17301512 | tf_op jit(solution)/shard_map/ppermute | solution.py:31
  873.4 184.2 %collective-permute-start.9 = (f32[512,1408]{1,0:T(8,128)}, f32[512,1408]{1,0:T(8,128)}, u32[]{:S(2)}, u32[]{:S(2)}) collective-permute-start(f32[512,1408]{1,0:T(8,128)} %dynamic-slice_bitcast_fusion.8), channel_id=1, source_target_pairs={{0,2},{1,3},{2,0},{3,1},{4,6},{5,7},{6,4},{7,5},{8,10},{9,11},{10,... | collective-permute-start | bytes 8650760 | tf_op jit(solution)/shard_map/ppermute | solution.py:31
  908.0 167.1 %collective-permute-start.8 = (f32[512,1408]{1,0:T(8,128)}, f32[512,1408]{1,0:T(8,128)}, u32[]{:S(2)}, u32[]{:S(2)}) collective-permute-start(f32[512,1408]{1,0:T(8,128)} %dynamic-slice_bitcast_fusion.9), channel_id=1, source_target_pairs={{0,4},{1,5},{2,6},{3,7},{4,0},{5,1},{6,2},{7,3},{8,12},{9,13},{10,... | collective-permute-start | bytes 8650760 | tf_op jit(solution)/shard_map/ppermute | solution.py:31
  1057.7 62.6 %collective-permute-start.15 = (f32[704,1024]{1,0:T(8,128)S(1)}, f32[704,1024]{1,0:T(8,128)S(1)}, u32[]{:S(2)}, u32[]{:S(2)}) collective-permute-start(f32[704,1024]{1,0:T(8,128)S(1)} %copy-done.8), channel_id=1, source_target_pairs={{0,8},{8,0},{1,9},{9,1},{2,10},{10,2},{3,11},{11,3},{4,12},{12,4},... | collective-permute-start | bytes 8650760 | tf_op jit(solution)/shard_map/ppermute | solution.py:34
  1126.9 61.8 %collective-permute-start.22 = (f32[512,1408]{1,0:T(8,128)S(1)}, f32[512,1408]{1,0:T(8,128)S(1)}, u32[]{:S(2)}, u32[]{:S(2)}) collective-permute-start(f32[512,1408]{1,0:T(8,128)S(1)} %dynamic-slice_bitcast_fusion.6), channel_id=1, source_target_pairs={{0,2},{1,3},{2,0},{3,1},{4,6},{5,7},{6,4},{7,5},{8,10},{9,11},{10,... | collective-permute-start | bytes 8650760 | tf_op jit(solution)/shard_map/ppermute | solution.py:31
  1137.5 61.8 %collective-permute-start.19 = (f32[512,1408]{1,0:T(8,128)}, f32[512,1408]{1,0:T(8,128)}, u32[]{:S(2)}, u32[]{:S(2)}) collective-permute-start(f32[512,1408]{1,0:T(8,128)} %dynamic-slice_bitcast_fusion.7), channel_id=1, source_target_pairs={{0,4},{1,5},{2,6},{3,7},{4,0},{5,1},{6,2},{7,3},{8,12},{9,13},{10,... | collective-permute-start | bytes 8650760 | tf_op jit(solution)/shard_map/ppermute | solution.py:31
  1138.1 67.2 %collective-permute-start.11 = (f32[512,1408]{1,0:T(8,128)}, f32[512,1408]{1,0:T(8,128)S(1)}, u32[]{:S(2)}, u32[]{:S(2)}) collective-permute-start(f32[512,1408]{1,0:T(8,128)} %bitcast_add_fusion.9), channel_id=1, source_target_pairs={{0,8},{8,0},{1,9},{9,1},{2,10},{10,2},{3,11},{11,3},{4,12},{12,4},... | collective-permute-start | bytes 8650760 | tf_op jit(solution)/shard_map/ppermute | solution.py:34
  1139.5 126.0 %collective-permute-start.12 = (f32[512,1408]{1,0:T(8,128)}, f32[512,1408]{1,0:T(8,128)}, u32[]{:S(2)}, u32[]{:S(2)}) collective-permute-start(f32[512,1408]{1,0:T(8,128)} %bitcast_add_fusion.8), channel_id=1, source_target_pairs={{0,8},{8,0},{1,9},{9,1},{2,10},{10,2},{3,11},{11,3},{4,12},{12,4},... | collective-permute-start | bytes 8650760 | tf_op jit(solution)/shard_map/ppermute | solution.py:34
  1190.5 136.8 %collective-permute-start.23 = (f32[512,1408]{1,0:T(8,128)}, f32[512,1408]{1,0:T(8,128)}, u32[]{:S(2)}, u32[]{:S(2)}) collective-permute-start(f32[512,1408]{1,0:T(8,128)} %bitcast_add_fusion.6), channel_id=1, source_target_pairs={{0,8},{8,0},{1,9},{9,1},{2,10},{10,2},{3,11},{11,3},{4,12},{12,4},... | collective-permute-start | bytes 8650760 | tf_op jit(solution)/shard_map/ppermute | solution.py:34
  1203.8 181.1 %collective-permute-start.20 = (f32[512,1408]{1,0:T(8,128)}, f32[512,1408]{1,0:T(8,128)}, u32[]{:S(2)}, u32[]{:S(2)}) collective-permute-start(f32[512,1408]{1,0:T(8,128)} %bitcast_add_fusion.7), channel_id=1, source_target_pairs={{0,8},{8,0},{1,9},{9,1},{2,10},{10,2},{3,11},{11,3},{4,12},{12,4},... | collective-permute-start | bytes 8650760 | tf_op jit(solution)/shard_map/ppermute | solution.py:34
  1269.7 63.4 %collective-permute-start.17 = (f32[256,1408]{1,0:T(8,128)}, f32[256,1408]{1,0:T(8,128)}, u32[]{:S(2)}, u32[]{:S(2)}) collective-permute-start(f32[256,1408]{1,0:T(8,128)} %constant_dynamic-slice_fusion.3), channel_id=1, source_target_pairs={{0,1},{1,0},{2,3},{3,2},{4,5},{5,4},{6,7},{7,6},{8,9},{9,8},{10,11... | collective-permute-start | bytes 4325384 | tf_op jit(solution)/shard_map/ppermute | solution.py:31
  1333.2 68.3 %collective-permute-start.24 = (f32[256,1408]{1,0:T(8,128)}, f32[256,1408]{1,0:T(8,128)}, u32[]{:S(2)}, u32[]{:S(2)}) collective-permute-start(f32[256,1408]{1,0:T(8,128)} %constant_dynamic-slice_fusion), channel_id=1, source_target_pairs={{0,1},{1,0},{2,3},{3,2},{4,5},{5,4},{6,7},{7,6},{8,9},{9,8},{10,11... | collective-permute-start | bytes 4325384 | tf_op jit(solution)/shard_map/ppermute | solution.py:31
  (22 other events, 491.0 us)
Sparse Core Ops, SparseCore 0:
  17.7 115.3 all-gather.3
  135.5 112.5 all-gather.5
  249.9 116.9 all-gather.7

commit v2 on v1

v2 whole, which is shorter than its diff:
```python
import jax
import jax.numpy as jnp
from jax import lax
from jax.sharding import PartitionSpec as P


NORM_EPS = 1e-5
F32 = jnp.float32
BF16 = jnp.bfloat16


def dot(a, b, da, db):
    return lax.dot_general(a, b, (((da,), (db,)), ((), ())), preferred_element_type=F32)


def after(value, *others):
    return lax.optimization_barrier((value, others))[0]


def pick(arr, idx, axis):
    return lax.dynamic_index_in_dim(arr, idx, axis, keepdims=False)


def solution(mesh):
    n_fsdp = mesh.shape['fsdp']
    tok_spec = P(('replica', 'fsdp'), None)
    act_spec = P(None, ('replica', 'fsdp'), None)
    weight_spec = P(None, 'fsdp', None)

    def swap(value, bit):
        return lax.ppermute(value, 'fsdp', [(i, i ^ bit) for i in range(n_fsdp)])

    def swap_z(value):
        return lax.ppermute(value, 'replica', [(0, 1), (1, 0)])

    def split_parity(w, blk):
        cols = [w[:, i * blk:(i + 1) * blk] for i in range(n_fsdp)]
        return jnp.concatenate(cols[0::2] + cols[1::2], axis=1)

    def local_step(block_in, grad_out, w_up, w_lin, w_down):
        layers, tok, dim = block_in.shape
        ff = w_up.shape[2]
        half = ff // 2
        rows = dim // n_fsdp
        ff_blk = ff // n_fsdp
        fi = lax.axis_index('fsdp').astype(jnp.uint32)
        core = (fi & 1).astype(jnp.int32)
        pos = (((fi >> 1) & 1).astype(jnp.int32), (fi >> 2).astype(jnp.int32))

        def slab1(g, first):
            g = g.reshape((2, 2) + g.shape[1:])
            return pick(g, 1 - pos[first], 1 - first)

        def send1(slab, first):
            return swap(slab, 2 << first)

        def add1(g, got, first):
            g = g.reshape((2, 2) + g.shape[1:])
            return pick(g, pos[first], 1 - first) + got

        def slab2(part, first):
            return pick(part, 1 - pos[1 - first], 0)

        def send2(slab, first):
            return swap(slab, 4 >> first)

        def add2(part, got, first):
            return pick(part, pos[1 - first], 0) + got

        def place_cols(halves):
            out = []
            for pieces in halves:
                evens, odds = [], []
                for tot in pieces:
                    mine = lax.dynamic_slice_in_dim(tot, core * rows, rows, axis=0)
                    other = lax.dynamic_slice_in_dim(tot, (1 - core) * rows, rows, axis=0)
                    got = swap(other, 1)
                    evens.append(jnp.where(core == 0, mine, got))
                    odds.append(jnp.where(core == 0, got, mine))
                even, odd = jnp.concatenate(evens, axis=1), jnp.concatenate(odds, axis=1)
                for j in range(even.shape[1] // ff_blk):
                    out += [even[:, j * ff_blk:(j + 1) * ff_blk], odd[:, j * ff_blk:(j + 1) * ff_blk]]
            return jnp.concatenate(out, axis=1)

        def take_cols(full):
            return lax.dynamic_slice_in_dim(full, core * (full.shape[1] // 2), full.shape[1] // 2, axis=1)

        grad_acc = grad_out.astype(F32)
        up_list = []
        lin_list = []
        down_list = []
        for l in reversed(range(layers)):
            up_eo = split_parity(w_up[l], ff_blk)
            lin_eo = split_parity(after(w_lin[l], up_eo), ff_blk)
            hc = half // 2
            up_w = take_cols(lax.all_gather(up_eo, 'fsdp', axis=0, tiled=True))
            lin_w = take_cols(lax.all_gather(lin_eo, 'fsdp', axis=0, tiled=True))
            down_w = lax.all_gather(after(w_down[l], lin_eo), 'fsdp', axis=0, tiled=True)
            down_w = pick(down_w.reshape(n_fsdp // 2, 2, ff_blk, dim), core, 1).reshape(2, hc, dim)
            h_f32 = block_in[l].astype(F32)
            inv_rms = lax.rsqrt(jnp.mean(h_f32 * h_f32, axis=-1, keepdims=True) + NORM_EPS)
            normed = h_f32 * inv_rms
            n_own = normed.astype(BF16)
            gb_own = grad_acc.astype(BF16)
            n = jnp.concatenate([n_own, swap(n_own, 1)], axis=0)
            gb = jnp.concatenate([gb_own, swap(gb_own, 1)], axis=0)

            pre_up = dot(n, up_w, 1, 0)
            pre_lin = dot(n, lin_w, 1, 0)
            act_b = (pre_up * jax.nn.sigmoid(pre_up) * pre_lin).astype(BF16)
            act_b, pre_up, pre_lin = lax.optimization_barrier((act_b, pre_up, pre_lin))

            hd = dim // 2
            down = [dot(act_b, gb[:, j * hd:(j + 1) * hd], 0, 0).reshape(4, ff_blk, hd) for j in range(2)]
            down_slab = [slab1(g, j) for j, g in enumerate(down)]
            down_got = [send1(g, j) for j, g in enumerate(down_slab)]

            def d_hidden(j, gb_j):
                u, v = pre_up[:, j * hc:(j + 1) * hc], pre_lin[:, j * hc:(j + 1) * hc]
                sig = jax.nn.sigmoid(u)
                d_act = dot(gb_j, down_w[j], 1, 1)
                d_u = (d_act * v * sig * (1.0 + u * (1.0 - sig))).astype(BF16)
                return d_u, (d_act * (u * sig)).astype(BF16)

            d_up0, d_lin0 = d_hidden(0, after(gb, down_slab))
            up0 = dot(n, d_up0, 0, 0).reshape(4, 2 * rows, hc)
            up_slab0 = slab1(up0, 0)
            up_got0 = send1(up_slab0, 0)
            down_got0 = after(down_got[0], up_slab0)
            down_part0 = add1(down[0], down_got0, 0)
            down_slab0 = slab2(down_part0, 0)
            down_got0 = send2(down_slab0, 0)
            d_up1, d_lin1 = d_hidden(1, after(gb, down_slab0))
            up1 = dot(n, d_up1, 0, 0).reshape(4, 2 * rows, hc)
            up_slab1 = slab1(up1, 1)
            up_got1 = send1(up_slab1, 1)
            down_got1 = after(down_got[1], up_slab1)
            down_part1 = add1(down[1], down_got1, 1)
            down_slab1 = slab2(down_part1, 1)
            down_got1 = send2(down_slab1, 1)
            edge = (hc // 256 + 1) * 128
            cut = [(0, edge), (edge, hc)]

            def lin_grad(n_late, d_l):
                return [dot(n_late, d_l[:, a:b], 0, 0).reshape(4, 2 * rows, b - a) for a, b in cut]

            lin0 = lin_grad(after(n, down_slab1), d_lin0)
            down_own0 = add2(down_part0, after(down_got0, lin0), 0)
            down_z0 = swap_z(down_own0)
            lin1 = lin_grad(after(n, down_own0), d_lin1)
            up_part0 = add1(up0, after(up_got0, lin1), 0)
            up_slab0 = slab2(up_part0, 0)
            up_got0 = send2(up_slab0, 0)
            lin0, lin1 = after((lin0, lin1), up_slab0)

            lin = list(zip(lin0, lin1))
            lin_slab = [slab1(lin[0][j], j) for j in range(2)]
            lin_got = [send1(lin_slab[j], j) for j in range(2)]
            down_own1 = add2(down_part1, after(down_got1, lin_slab), 1)
            down_z1 = swap_z(down_own1)

            d_up_late = after((d_up0, d_up1, d_lin0, d_lin1), down_own1)

            def d_norm_of(parts, sl):
                u0, u1, l0, l1 = [p[sl] for p in parts]
                return (dot(u0, up_w[:, :hc], 1, 1) + dot(u1, up_w[:, hc:], 1, 1)
                        + dot(l0, lin_w[:, :hc], 1, 1) + dot(l1, lin_w[:, hc:], 1, 1))

            d_norm_par = d_norm_of(d_up_late, slice(tok, 2 * tok))
            d_norm_got = swap(d_norm_par, 1)
            up_part1 = add1(up1, after(up_got1, d_norm_par), 1)
            up_slab1 = slab2(up_part1, 1)
            up_got1 = send2(up_slab1, 1)
            up_own0 = add2(up_part0, after(up_got0, up_slab1), 0)
            up_z0 = swap_z(up_own0)
            d_norm = d_norm_of(after(d_up_late, up_own0), slice(0, tok)) + d_norm_got
            up_own1 = add2(up_part1, after(up_got1, d_norm), 1)
            up_z1 = swap_z(up_own1)
            lin_part = [add1(lin[0][j], after(lin_got[j], up_own1), j) for j in range(2)]
            lin_slab = [slab2(lin_part[j], j) for j in range(2)]
            lin_got = [send2(lin_slab[j], j) for j in range(2)]
            lin_b_slab = [slab1(after(lin[1][j], lin_slab), j) for j in range(2)]
            lin_b_got = [send1(lin_b_slab[j], j) for j in range(2)]
            d_norm = after(d_norm, lin_b_slab)
            d_h = inv_rms * (d_norm - normed * jnp.mean(d_norm * normed, axis=-1, keepdims=True))
            grad_acc = grad_acc + d_h
            lin_own = [add2(lin_part[j], after(lin_got[j], lin_b_slab), j) for j in range(2)]
            lin_z = [swap_z(v) for v in lin_own]
            lin_b_part = [add1(lin[1][j], after(lin_b_got[j], lin_own), j) for j in range(2)]
            lin_b_slab = [slab2(lin_b_part[j], j) for j in range(2)]
            lin_b_got = [send2(lin_b_slab[j], j) for j in range(2)]
            lin_b_own = [add2(lin_b_part[j], lin_b_got[j], j) for j in range(2)]
            lin_b_z = [swap_z(v) for v in lin_b_own]
            down_z0, down_z1, up_z0, up_z1, lin_z = after((down_z0, down_z1, up_z0, up_z1, lin_z), lin_b_own)
            down_sum = [down_own0 + down_z0, down_own1 + down_z1]
            up_sum = [[up_own0 + up_z0], [up_own1 + up_z1]]
            lin_sum = [lin_own[j] + lin_z[j] for j in range(2)]
            down_list.insert(0, jnp.concatenate(down_sum, axis=1))
            up_list.insert(0, place_cols(up_sum))
            lin_b_z = after(lin_b_z, up_list[0], down_list[0])
            lin_list.insert(0, place_cols([[lin_sum[j], lin_b_own[j] + lin_b_z[j]] for j in range(2)]))
        return jnp.stack(up_list), jnp.stack(lin_list), jnp.stack(down_list), grad_acc.astype(BF16)

    return jax.shard_map(local_step, mesh=mesh, in_specs=(act_spec, tok_spec, weight_spec, weight_spec, weight_spec), out_specs=(weight_spec, weight_spec, weight_spec, tok_spec), check_vma=False)
```

time: 1430 us -> 1550 us (1.084)
  matrix products: 541 us -> 603 us
  waiting for transfers between devices: 591 us -> 650 us
    dot_general x13 -> x20, matrix products: 541 us -> 603 us  [dot(): lax.dot_general(a, b, (((da,), (db,)), ((), ())), preferred_element_type=...]
    ppermute x6 -> x8, waiting for transfers between devices: 184 us -> 240 us  [swap_z(): return lax.ppermute(value, 'replica', [(0, 1), (1, 0)])]
    add x7 -> x8, other arithmetic: 35.1 us -> 15.8 us  [the longest x2 7.04 us: local_step(): up_sum = [[up_own0 + up_z0], [up_own1 + up_z1]]]
    squeeze x12 -> x16, local copies, waits for them, and re-layouts: 42.8 us -> 35.6 us  [pick(): return lax.dynamic_index_in_dim(arr, idx, axis, keepdims=False)]
    ppermute x19 -> x25, waiting for transfers between devices: 298 us -> 300 us  [swap(): return lax.ppermute(value, 'fsdp', [(i, i ^ bit) for i in range(n_fsdp)])]
  transfers between devices with their start and end apart: 28 -> 36, of which waited for: 12 -> 18; matrix products, arithmetic and copies ran while one was open for 46% -> 47% of each run, Pallas kernels for 0% -> 0%
where the time goes in v2:
time: 1550 us; the launch traced here: 1540 us
  waiting for transfers between devices  650 us (42%)
  matrix products  603 us (39%)
  other arithmetic  127 us (8%)
  local copies, waits for them, and re-layouts  121 us (8%)
  starting transfers between devices  25.8 us (2%)
    dot_general x20, matrix products, dot(): lax.dot_general(a, b, (((da,), (db,)), ((), ())), preferred_element_type=...  603 us
    ppermute x25, waiting for transfers between devices, swap(): return lax.ppermute(value, 'fsdp', [(i, i ^ bit) for i in range(n_fsdp)])  300 us
    ppermute x8, waiting for transfers between devices, swap_z(): return lax.ppermute(value, 'replica', [(0, 1), (1, 0)])  240 us
    all_gather x1, waiting for transfers between devices, local_step(): lin_w = take_cols(lax.all_gather(lin_eo, 'fsdp', axis=0, tiled=True))  56 us
    all_gather x1, waiting for transfers between devices, local_step(): up_w = take_cols(lax.all_gather(up_eo, 'fsdp', axis=0, tiled=True))  53.5 us
    squeeze x16, local copies, waits for them, and re-layouts, pick(): return lax.dynamic_index_in_dim(arr, idx, axis, keepdims=False)  35.6 us
  transfers between devices with their start and end apart: 36, of which 18 were waited for; matrix products, arithmetic and copies ran while one was open for 47% of the time, Pallas kernels for 0%

profile of v2, /device:TPU:0, one launch (start us, length us, event | category | flops | bytes accessed | tf_op | source)
XLA Modules:
  0.0 1541.4 jit_solution(3699225144205351844)
XLA Ops:
  79.5 53.5 %all-gather.4.cloned.1.call-done = bf16[2048,5632]{1,0:T(8,128)(2,1)} async-done(((bf16[256,5632]{1,0:T(8,128)(2,1)}), bf16[2048,5632]{1,0:T(8,128)(2,1)}) %all-gather.4.cloned.1.call-update) | async-done | bytes 23068688 | tf_op jit(solution)/shard_map/all_gather | solution.py:96
  133.1 59.0 %fusion.11 = f32[4096,2816]{1,0:T(8,128)} fusion(bf16[2048,5632]{1,0:T(8,128)(2,1)} %all-gather.4.cloned.1.call-done, s32[]{:T(128)S(6)} %select_n.137, bf16[2048,2048]{1,0:T(8,128)(2,1)} %collective-permute-done, bf16[2048,2048]{1,0:T(8,128)(2,1)} %fusion.2), kind=kOutput, calls=%fused_computation.23 | convolution fusion | flops 47278194688 | bytes 74448896 | tf_op jit(solution)/shard_map/dot_general | solution.py:13
  192.1 56.0 %all-gather.6.cloned.1.call-done = bf16[2048,5632]{1,0:T(8,128)(2,1)} async-done(((bf16[256,5632]{1,0:T(8,128)(2,1)}), bf16[2048,5632]{1,0:T(8,128)(2,1)}) %all-gather.6.cloned.1.call-update) | async-done | bytes 23068688 | tf_op jit(solution)/shard_map/all_gather | solution.py:97
  248.1 63.8 %multiply_convert_fusion = (bf16[4096,2816]{1,0:T(8,128)(2,1)}, f32[4096,2816]{1,0:T(8,128)}) fusion(f32[4096,2816]{1,0:T(8,128)} %fusion.11, bf16[2048,5632]{1,0:T(8,128)(2,1)} %all-gather.6.cloned.1.call-done, s32[]{:T(128)S(6)} %select_n.137, bf16[2048,2048]{1,0:T(8,128)(2,1)} %collective-permute-done, bf16[2048,2048]{1,0:T(8,128)(2,1)} %fusion.2), kind=kOutput, calls=%fused_computation | convolution fusion | flops 47347400704 | bytes 143654912 | tf_op jit(solution)/shard_map/dot_general | solution.py:13
  311.9 34.0 %fusion.15 = f32[2816,1024]{1,0:T(8,128)} fusion(bf16[4096,2816]{1,0:T(8,128)(2,1)} %get-tuple-element.51, bf16[4096,2048]{1,0:T(8,128)(2,1)} %constant_dynamic-update-slice_fusion), kind=kOutput, calls=%fused_computation.27 | convolution fusion | flops 23622320128 | bytes 42991616 | tf_op jit(solution)/shard_map/dot_general | solution.py:13
  353.3 34.2 %fusion.13 = f32[2816,1024]{1,0:T(8,128)} fusion(bf16[4096,2816]{1,0:T(8,128)(2,1)} %get-tuple-element.51, bf16[4096,2048]{1,0:T(8,128)(2,1)} %constant_dynamic-update-slice_fusion), kind=kOutput, calls=%fused_computation.25 | convolution fusion | flops 23622320128 | bytes 42991616 | tf_op jit(solution)/shard_map/dot_general | solution.py:13
  405.4 41.4 %multiply_convert_fusion.2 = (bf16[4096,1408]{1,0:T(8,128)(2,1)}, bf16[4096,1408]{1,0:T(8,128)(2,1)}) fusion(f32[4096,2816]{1,0:T(8,128)} %fusion.11, f32[4096,2816]{1,0:T(8,128)} %get-tuple-element.54, bf16[4096,2048]{1,0:T(8,128)(2,1)} %constant_dynamic-update-slice_fusion, bf16[1408,2048]{1,0:T(8,128)(2,1)} %bitcast.130), kind=kOutput, calls=%fused_computation.2 | convolution fusion | flops 23697293312 | bytes 91750400 | tf_op jit(solution)/shard_map/dot_general | solution.py:13
  446.7 33.2 %fusion.59 = f32[2048,1408]{1,0:T(8,128)S(1)} fusion(bf16[4096,1408]{1,0:T(8,128)(2,1)} %get-tuple-element.72, bf16[2048,2048]{1,0:T(8,128)(2,1)} %collective-permute-done, bf16[2048,2048]{1,0:T(8,128)(2,1)} %fusion.2), kind=kOutput, calls=%fused_computation.132 | convolution fusion | flops 23655874560 | bytes 39845888 | tf_op jit(solution)/shard_map/dot_general | solution.py:13
  497.4 41.6 %multiply_convert_fusion.1 = (bf16[4096,1408]{1,0:T(8,128)(2,1)}, bf16[4096,1408]{1,0:T(8,128)(2,1)}) fusion(f32[4096,2816]{1,0:T(8,128)} %fusion.11, f32[4096,2816]{1,0:T(8,128)} %get-tuple-element.54, bf16[4096,2048]{1,0:T(8,128)(2,1)} %constant_dynamic-update-slice_fusion, bf16[1408,2048]{1,0:T(8,128)(2,1)} %bitcast.129), kind=kOutput, calls=%fused_computation.1 | convolution fusion | flops 23697293312 | bytes 91750400 | tf_op jit(solution)/shard_map/dot_general | solution.py:13
  539.0 33.5 %fusion.58 = f32[2048,1408]{1,0:T(8,128)S(1)} fusion(bf16[4096,1408]{1,0:T(8,128)(2,1)} %get-tuple-element.73, bf16[2048,2048]{1,0:T(8,128)(2,1)} %collective-permute-done, bf16[2048,2048]{1,0:T(8,128)(2,1)} %fusion.2), kind=kOutput, calls=%fused_computation.131 | convolution fusion | flops 23655874560 | bytes 39845888 | tf_op jit(solution)/shard_map/dot_general | solution.py:13
  604.5 21.0 %fusion.37 = f32[2048,640]{1,0:T(8,128)} fusion(bf16[4096,2048]{1,0:T(8,128)(2,1)} %pad_maximum_fusion, bf16[4096,1408]{1,0:T(8,128)(2,1)} %get-tuple-element.74), kind=kOutput, calls=%fused_computation.58 | convolution fusion | flops 10737418240 | bytes 27262976 | tf_op jit(solution)/shard_map/dot_general | solution.py:13
  630.6 21.1 %fusion.17 = f32[2048,768]{1,0:T(8,128)} fusion(bf16[4096,2048]{1,0:T(8,128)(2,1)} %pad_maximum_fusion, bf16[4096,1408]{1,0:T(8,128)(2,1)} %get-tuple-element.75), kind=kOutput, calls=%fused_computation.29 | convolution fusion | flops 12884901888 | bytes 29360128 | tf_op jit(solution)/shard_map/dot_general | solution.py:13
  752.1 30.3 %add_add_fusion.1 = f32[2048,2048]{1,0:T(8,128)} fusion(f32[2048,2048]{1,0:T(8,128)} %fusion.29, f32[2048,2048]{1,0:T(8,128)} %fusion.33, f32[2048,2048]{1,0:T(8,128)} %fusion.31, bf16[4096,1408]{1,0:T(8,128)(2,1)} %get-tuple-element.75, bf16[2048,5632]{1,0:T(8,128)(2,1)} %all-gather.6.cloned.1.call-done, s32[]{:T(128)S(6)} %add.248), kind=kOutput, calls=%fused_computation.20 | convolution fusion | flops 11823742976 | bytes 78643200 | tf_op jit(solution)/shard_map/dot_general | solution.py:13
  785.5 124.2 %collective-permute-done.7 = f32[2,512,1408]{2,1,0:T(8,128)S(1)} collective-permute-done((f32[2,512,1408]{2,1,0:T(8,128)}, f32[2,512,1408]{2,1,0:T(8,128)S(1)}, u32[]{:S(2)}, u32[]{:S(2)}) %collective-permute-start.7) | collective-permute-done | bytes 5767200 | tf_op jit(solution)/shard_map/ppermute | solution.py:31
  916.0 55.6 %collective-permute-done.6 = f32[512,1408]{1,0:T(8,128)S(1)} collective-permute-done((f32[512,1408]{1,0:T(8,128)}, f32[512,1408]{1,0:T(8,128)S(1)}, u32[]{:S(2)}, u32[]{:S(2)}) %collective-permute-start.6) | collective-permute-done | bytes 2883616 | tf_op jit(solution)/shard_map/ppermute | solution.py:31
  1033.6 36.5 %add_add_fusion = f32[2048,2048]{1,0:T(8,128)} fusion(f32[2048,2048]{1,0:T(8,128)} %collective-permute-done.13, f32[2048,2048]{1,0:T(8,128)} %fusion.22, f32[2048,2048]{1,0:T(8,128)} %fusion.26, f32[2048,2048]{1,0:T(8,128)} %fusion.24, bf16[4096,1408]{1,0:T(8,128)(2,1)} %get-tuple-element.75, bf16[2048,5632]{1,0:T(8,128)(2,1)} %all-gather.6.cloned.1.call-done, ...), kind=kOutput, calls=%fused_computation.19 | convolution fusion | flops 11827937280 | bytes 95420416 | tf_op jit(solution)/shard_map/dot_general | solution.py:13
  1088.8 32.0 %collective-permute-done.19 = f32[512,768]{1,0:T(8,128)S(1)} collective-permute-done((f32[512,768]{1,0:T(8,128)S(1)}, f32[512,768]{1,0:T(8,128)S(1)}, u32[]{:S(2)}, u32[]{:S(2)}) %collective-permute-start.19) | collective-permute-done | bytes 1572896 | tf_op jit(solution)/shard_map/ppermute | solution.py:31
  1120.8 54.0 %collective-permute-done.16 = f32[512,768]{1,0:T(8,128)S(1)} collective-permute-done((f32[512,768]{1,0:T(8,128)S(1)}, f32[512,768]{1,0:T(8,128)S(1)}, u32[]{:S(2)}, u32[]{:S(2)}) %collective-permute-start.16) | collective-permute-done | bytes 1572896 | tf_op jit(solution)/shard_map/ppermute | solution.py:31
  1187.0 21.6 %collective-permute-done.24 = f32[512,640]{1,0:T(8,128)} collective-permute-done((f32[512,640]{1,0:T(8,128)}, f32[512,640]{1,0:T(8,128)}, u32[]{:S(2)}, u32[]{:S(2)}) %collective-permute-start.24) | collective-permute-done | bytes 1310752 | tf_op jit(solution)/shard_map/ppermute | solution.py:31
  1247.3 61.8 %collective-permute-done.11 = f32[512,1408]{1,0:T(8,128)} collective-permute-done((f32[512,1408]{1,0:T(8,128)}, f32[512,1408]{1,0:T(8,128)}, u32[]{:S(2)}, u32[]{:S(2)}) %collective-permute-start.11) | collective-permute-done | bytes 2883616 | tf_op jit(solution)/shard_map/ppermute | solution.py:34
  1309.1 61.8 %collective-permute-done.14 = f32[512,1408]{1,0:T(8,128)} collective-permute-done((f32[512,1408]{1,0:T(8,128)}, f32[512,1408]{1,0:T(8,128)}, u32[]{:S(2)}, u32[]{:S(2)}) %collective-permute-start.14) | collective-permute-done | bytes 2883616 | tf_op jit(solution)/shard_map/ppermute | solution.py:34
  1370.9 33.6 %collective-permute-done.20 = f32[512,768]{1,0:T(8,128)S(1)} collective-permute-done((f32[512,768]{1,0:T(8,128)}, f32[512,768]{1,0:T(8,128)S(1)}, u32[]{:S(2)}, u32[]{:S(2)}) %collective-permute-start.20) | collective-permute-done | bytes 1572896 | tf_op jit(solution)/shard_map/ppermute | solution.py:34
  1404.5 31.3 %collective-permute-done.18 = f32[512,768]{1,0:T(8,128)S(1)} collective-permute-done((f32[512,768]{1,0:T(8,128)}, f32[512,768]{1,0:T(8,128)S(1)}, u32[]{:S(2)}, u32[]{:S(2)}) %collective-permute-start.18) | collective-permute-done | bytes 1572896 | tf_op jit(solution)/shard_map/ppermute | solution.py:34
  1488.3 27.6 %collective-permute-done.28 = f32[512,640]{1,0:T(8,128)} collective-permute-done((f32[512,640]{1,0:T(8,128)}, f32[512,640]{1,0:T(8,128)}, u32[]{:S(2)}, u32[]{:S(2)}) %collective-permute-start.28) | collective-permute-done | bytes 1310752 | tf_op jit(solution)/shard_map/ppermute | solution.py:34
  (251 shorter events, 464.1 us)
Async XLA Ops:
  7.2 125.9 %all-gather.4.cloned.1.call-start = ((), (), s32[]{:S(2)}) async-start(), calls=%async_computation | async-start | bytes 25952256 | tf_op jit(solution)/shard_map/all_gather | solution.py:96
  17.5 230.6 %all-gather.6.cloned.1.call-start = ((), (), s32[]{:S(2)}) async-start(), calls=%async_computation.1 | async-start | bytes 25952256 | tf_op jit(solution)/shard_map/all_gather | solution.py:97
  25.8 368.3 %all-gather.8.cloned.1.call-start = ((), (), s32[]{:S(2)}) async-start(), calls=%async_computation.2 | async-start | bytes 25952256 | tf_op jit(solution)/shard_map/all_gather | solution.py:98
  352.1 133.8 %collective-permute-start.3 = (f32[2,704,1024]{2,1,0:T(8,128)}, f32[2,704,1024]{2,1,0:T(8,128)}, u32[]{:S(2)}, u32[]{:S(2)}) collective-permute-start(f32[2,704,1024]{2,1,0:T(8,128)} %dynamic-slice_bitcast_fusion.3), channel_id=1, source_target_pairs={{0,2},{1,3},{2,0},{3,1},{4,6},{5,7},{6,4},{7,5},{8,10},{9,11},{10,... | collective-permute-start | bytes 17301512 | tf_op jit(solution)/shard_map/ppermute | solution.py:31
  393.6 184.8 %collective-permute-start.5 = (f32[2,704,1024]{2,1,0:T(8,128)}, f32[2,704,1024]{2,1,0:T(8,128)}, u32[]{:S(2)}, u32[]{:S(2)}) collective-permute-start(f32[2,704,1024]{2,1,0:T(8,128)} %dynamic-slice_bitcast_fusion.2), channel_id=1, source_target_pairs={{0,4},{1,5},{2,6},{3,7},{4,0},{5,1},{6,2},{7,3},{8,12},{9,13},{10,... | collective-permute-start | bytes 17301512 | tf_op jit(solution)/shard_map/ppermute | solution.py:31
  483.1 187.3 %collective-permute-start.2 = (f32[2,512,1408]{2,1,0:T(8,128)}, f32[2,512,1408]{2,1,0:T(8,128)}, u32[]{:S(2)}, u32[]{:S(2)}) collective-permute-start(f32[2,512,1408]{2,1,0:T(8,128)} %dynamic-slice_bitcast_fusion.1), channel_id=1, source_target_pairs={{0,2},{1,3},{2,0},{3,1},{4,6},{5,7},{6,4},{7,5},{8,10},{9,11},{10,... | collective-permute-start | bytes 17301512 | tf_op jit(solution)/shard_map/ppermute | solution.py:31
  495.9 130.6 %collective-permute-start.4 = (f32[704,1024]{1,0:T(8,128)}, f32[704,1024]{1,0:T(8,128)}, u32[]{:S(2)}, u32[]{:S(2)}) collective-permute-start(f32[704,1024]{1,0:T(8,128)} %dynamic-slice_bitcast_fusion.9), channel_id=1, source_target_pairs={{0,4},{1,5},{2,6},{3,7},{4,0},{5,1},{6,2},{7,3},{8,12},{9,13},{10,... | collective-permute-start | bytes 8650760 | tf_op jit(solution)/shard_map/ppermute | solution.py:31
  625.5 64.2 %collective-permute-start.8 = (f32[704,1024]{1,0:T(8,128)}, f32[704,1024]{1,0:T(8,128)}, u32[]{:S(2)}, u32[]{:S(2)}) collective-permute-start(f32[704,1024]{1,0:T(8,128)} %dynamic-slice_bitcast_fusion.8), channel_id=1, source_target_pairs={{0,2},{1,3},{2,0},{3,1},{4,6},{5,7},{6,4},{7,5},{8,10},{9,11},{10,... | collective-permute-start | bytes 8650760 | tf_op jit(solution)/shard_map/ppermute | solution.py:31
  782.4 251.3 %collective-permute-start.13 = (f32[2048,2048]{1,0:T(8,128)}, f32[2048,2048]{1,0:T(8,128)}, u32[]{:S(2)}, u32[]{:S(2)}) collective-permute-start(f32[2048,2048]{1,0:T(8,128)} %add_add_fusion.1), channel_id=1, source_target_pairs={{0,1},{1,0},{2,3},{3,2},{4,5},{5,4},{6,7},{7,6},{8,9},{9,8},{10,11... | collective-permute-start | bytes 50331656 | tf_op jit(solution)/shard_map/ppermute | solution.py:31
  782.4 127.4 %collective-permute-start.7 = (f32[2,512,1408]{2,1,0:T(8,128)}, f32[2,512,1408]{2,1,0:T(8,128)S(1)}, u32[]{:S(2)}, u32[]{:S(2)}) collective-permute-start(f32[2,512,1408]{2,1,0:T(8,128)} %dynamic-slice_bitcast_fusion), channel_id=1, source_target_pairs={{0,4},{1,5},{2,6},{3,7},{4,0},{5,1},{6,2},{7,3},{8,12},{9,13},{10,... | collective-permute-start | bytes 17301512 | tf_op jit(solution)/shard_map/ppermute | solution.py:31
  782.9 188.7 %collective-permute-start.6 = (f32[512,1408]{1,0:T(8,128)}, f32[512,1408]{1,0:T(8,128)S(1)}, u32[]{:S(2)}, u32[]{:S(2)}) collective-permute-start(f32[512,1408]{1,0:T(8,128)} %dynamic-slice_bitcast_fusion.7), channel_id=1, source_target_pairs={{0,4},{1,5},{2,6},{3,7},{4,0},{5,1},{6,2},{7,3},{8,12},{9,13},{10,... | collective-permute-start | bytes 8650760 | tf_op jit(solution)/shard_map/ppermute | solution.py:31
  784.4 290.5 %collective-permute-start.17 = (f32[2,512,768]{2,1,0:T(8,128)}, f32[2,512,768]{2,1,0:T(8,128)}, u32[]{:S(2)}, u32[]{:S(2)}) collective-permute-start(f32[2,512,768]{2,1,0:T(8,128)} %dynamic-slice_bitcast_fusion.4), channel_id=1, source_target_pairs={{0,4},{1,5},{2,6},{3,7},{4,0},{5,1},{6,2},{7,3},{8,12},{9,13},{10,... | collective-permute-start | bytes 9437192 | tf_op jit(solution)/shard_map/ppermute | solution.py:31
  784.9 293.5 %collective-permute-start.15 = (f32[2,512,768]{2,1,0:T(8,128)S(1)}, f32[2,512,768]{2,1,0:T(8,128)}, u32[]{:S(2)}, u32[]{:S(2)}) collective-permute-start(f32[2,512,768]{2,1,0:T(8,128)S(1)} %copy-done.19), channel_id=1, source_target_pairs={{0,2},{1,3},{2,0},{3,1},{4,6},{5,7},{6,4},{7,5},{8,10},{9,11},{10,... | collective-permute-start | bytes 9437192 | tf_op jit(solution)/shard_map/ppermute | solution.py:31
  915.2 155.0 %collective-permute-start.12 = (f32[512,1408]{1,0:T(8,128)}, f32[512,1408]{1,0:T(8,128)}, u32[]{:S(2)}, u32[]{:S(2)}) collective-permute-start(f32[512,1408]{1,0:T(8,128)} %dynamic-slice_bitcast_fusion.6), channel_id=1, source_target_pairs={{0,2},{1,3},{2,0},{3,1},{4,6},{5,7},{6,4},{7,5},{8,10},{9,11},{10,... | collective-permute-start | bytes 8650760 | tf_op jit(solution)/shard_map/ppermute | solution.py:31
  1083.0 94.7 %collective-permute-start.23 = (f32[2,512,640]{2,1,0:T(8,128)S(1)}, f32[2,512,640]{2,1,0:T(8,128)S(1)}, u32[]{:S(2)}, u32[]{:S(2)}) collective-permute-start(f32[2,512,640]{2,1,0:T(8,128)S(1)} %dynamic-slice_bitcast_fusion.10), channel_id=1, source_target_pairs={{0,4},{1,5},{2,6},{3,7},{4,0},{5,1},{6,2},{7,3},{8,12},{9,13},{10,... | collective-permute-start | bytes 7864328 | tf_op jit(solution)/shard_map/ppermute | solution.py:31
  1084.2 90.7 %collective-permute-start.16 = (f32[512,768]{1,0:T(8,128)S(1)}, f32[512,768]{1,0:T(8,128)S(1)}, u32[]{:S(2)}, u32[]{:S(2)}) collective-permute-start(f32[512,768]{1,0:T(8,128)S(1)} %dynamic-slice_bitcast_fusion.13), channel_id=1, source_target_pairs={{0,4},{1,5},{2,6},{3,7},{4,0},{5,1},{6,2},{7,3},{8,12},{9,13},{10,... | collective-permute-start | bytes 4718600 | tf_op jit(solution)/shard_map/ppermute | solution.py:31
  1086.1 93.9 %collective-permute-start.21 = (f32[2,512,640]{2,1,0:T(8,128)S(1)}, f32[2,512,640]{2,1,0:T(8,128)S(1)}, u32[]{:S(2)}, u32[]{:S(2)}) collective-permute-start(f32[2,512,640]{2,1,0:T(8,128)S(1)} %dynamic-slice_bitcast_fusion.11), channel_id=1, source_target_pairs={{0,2},{1,3},{2,0},{3,1},{4,6},{5,7},{6,4},{7,5},{8,10},{9,11},{10,... | collective-permute-start | bytes 7864328 | tf_op jit(solution)/shard_map/ppermute | solution.py:31
  1087.4 96.5 %collective-permute-start.10 = (f32[704,1024]{1,0:T(8,128)S(1)}, f32[704,1024]{1,0:T(8,128)S(1)}, u32[]{:S(2)}, u32[]{:S(2)}) collective-permute-start(f32[704,1024]{1,0:T(8,128)S(1)} %copy-done.8), channel_id=1, source_target_pairs={{0,8},{8,0},{1,9},{9,1},{2,10},{10,2},{3,11},{11,3},{4,12},{12,4},... | collective-permute-start | bytes 8650760 | tf_op jit(solution)/shard_map/ppermute | solution.py:34
  1181.8 65.5 %collective-permute-start.9 = (f32[704,1024]{1,0:T(8,128)S(1)}, f32[704,1024]{1,0:T(8,128)}, u32[]{:S(2)}, u32[]{:S(2)}) collective-permute-start(f32[704,1024]{1,0:T(8,128)S(1)} %copy-done.7), channel_id=1, source_target_pairs={{0,8},{8,0},{1,9},{9,1},{2,10},{10,2},{3,11},{11,3},{4,12},{12,4},... | collective-permute-start | bytes 8650760 | tf_op jit(solution)/shard_map/ppermute | solution.py:34
  1183.4 125.7 %collective-permute-start.11 = (f32[512,1408]{1,0:T(8,128)}, f32[512,1408]{1,0:T(8,128)}, u32[]{:S(2)}, u32[]{:S(2)}) collective-permute-start(f32[512,1408]{1,0:T(8,128)} %bitcast_add_fusion.8), channel_id=1, source_target_pairs={{0,8},{8,0},{1,9},{9,1},{2,10},{10,2},{3,11},{11,3},{4,12},{12,4},... | collective-permute-start | bytes 8650760 | tf_op jit(solution)/shard_map/ppermute | solution.py:34
  1185.4 185.4 %collective-permute-start.14 = (f32[512,1408]{1,0:T(8,128)}, f32[512,1408]{1,0:T(8,128)}, u32[]{:S(2)}, u32[]{:S(2)}) collective-permute-start(f32[512,1408]{1,0:T(8,128)} %bitcast_add_fusion.6), channel_id=1, source_target_pairs={{0,8},{8,0},{1,9},{9,1},{2,10},{10,2},{3,11},{11,3},{4,12},{12,4},... | collective-permute-start | bytes 8650760 | tf_op jit(solution)/shard_map/ppermute | solution.py:34
  1208.6 195.8 %collective-permute-start.20 = (f32[512,768]{1,0:T(8,128)}, f32[512,768]{1,0:T(8,128)S(1)}, u32[]{:S(2)}, u32[]{:S(2)}) collective-permute-start(f32[512,768]{1,0:T(8,128)} %bitcast_add_fusion.12), channel_id=1, source_target_pairs={{0,8},{8,0},{1,9},{9,1},{2,10},{10,2},{3,11},{11,3},{4,12},{12,4},... | collective-permute-start | bytes 4718600 | tf_op jit(solution)/shard_map/ppermute | solution.py:34
  1210.7 225.1 %collective-permute-start.18 = (f32[512,768]{1,0:T(8,128)}, f32[512,768]{1,0:T(8,128)S(1)}, u32[]{:S(2)}, u32[]{:S(2)}) collective-permute-start(f32[512,768]{1,0:T(8,128)} %bitcast_add_fusion.13), channel_id=1, source_target_pairs={{0,8},{8,0},{1,9},{9,1},{2,10},{10,2},{3,11},{11,3},{4,12},{12,4},... | collective-permute-start | bytes 4718600 | tf_op jit(solution)/shard_map/ppermute | solution.py:34
  1457.8 58.1 %collective-permute-start.28 = (f32[512,640]{1,0:T(8,128)}, f32[512,640]{1,0:T(8,128)}, u32[]{:S(2)}, u32[]{:S(2)}) collective-permute-start(f32[512,640]{1,0:T(8,128)} %bitcast_add_fusion.15), channel_id=1, source_target_pairs={{0,8},{8,0},{1,9},{9,1},{2,10},{10,2},{3,11},{11,3},{4,12},{12,4},... | collective-permute-start | bytes 3932168 | tf_op jit(solution)/shard_map/ppermute | solution.py:34
  (60 other events, 1776.9 us)
Sparse Core Ops, SparseCore 0:
  17.7 115.3 all-gather.3
  135.5 112.5 all-gather.5
  249.9 116.0 all-gather.7

commit v3 on v2

--- a/solution.py
+++ b/solution.py
@@ -159,36 +159,38 @@
             down_own1 = add2(down_part1, after(down_got1, lin_slab), 1)
             down_z1 = swap_z(down_own1)
 
-            d_up_late = after((d_up0, d_up1, d_lin0, d_lin1), down_own1)
-
-            def d_norm_of(parts, sl):
-                u0, u1, l0, l1 = [p[sl] for p in parts]
-                return (dot(u0, up_w[:, :hc], 1, 1) + dot(u1, up_w[:, hc:], 1, 1)
-                        + dot(l0, lin_w[:, :hc], 1, 1) + dot(l1, lin_w[:, hc:], 1, 1))
-
-            d_norm_par = d_norm_of(d_up_late, slice(tok, 2 * tok))
-            d_norm_got = swap(d_norm_par, 1)
-            up_part1 = add1(up1, after(up_got1, d_norm_par), 1)
+            up_part1 = add1(up1, after(up_got1, down_own1), 1)
             up_slab1 = slab2(up_part1, 1)
             up_got1 = send2(up_slab1, 1)
-            up_own0 = add2(up_part0, after(up_got0, up_slab1), 0)
+
+            def d_norm_term(i, sl, *earlier):
+                d = after((d_up0, d_up1, d_lin0, d_lin1)[i], *earlier)[sl]
+                return dot(d, (up_w, lin_w)[i // 2][:, (i % 2) * hc:(i % 2 + 1) * hc], 1, 1)
+
+            theirs, ours = slice(tok, 2 * tok), slice(0, tok)
+            d_norm_par = sum(d_norm_term(i, theirs, up_slab1) for i in range(1, 3)) + d_norm_term(0, theirs, up_slab1)
+            up_own0 = add2(up_part0, after(up_got0, d_norm_par), 0)
             up_z0 = swap_z(up_own0)
-            d_norm = d_norm_of(after(d_up_late, up_own0), slice(0, tok)) + d_norm_got
+            lin_b_slab = [slab1(after(lin[1][j], up_own0), j) for j in range(2)]
+            lin_b_got = [send1(lin_b_slab[j], j) for j in range(2)]
+            d_norm_par = after(d_norm_par, lin_b_slab) + d_norm_term(3, theirs, lin_b_slab)
+            d_norm_got = swap(d_norm_par, 1)
+            d_norm = d_norm_term(0, ours, d_norm_par)
             up_own1 = add2(up_part1, after(up_got1, d_norm), 1)
             up_z1 = swap_z(up_own1)
             lin_part = [add1(lin[0][j], after(lin_got[j], up_own1), j) for j in range(2)]
             lin_slab = [slab2(lin_part[j], j) for j in range(2)]
             lin_got = [send2(lin_slab[j], j) for j in range(2)]
-            lin_b_slab = [slab1(after(lin[1][j], lin_slab), j) for j in range(2)]
-            lin_b_got = [send1(lin_b_slab[j], j) for j in range(2)]
-            d_norm = after(d_norm, lin_b_slab)
+            d_norm = d_norm + d_norm_term(1, ours, lin_slab) + d_norm_term(2, ours, lin_slab)
+            lin_b_part = [add1(lin[1][j], after(lin_b_got[j], d_norm), j) for j in range(2)]
+            lin_b_slab = [slab2(lin_b_part[j], j) for j in range(2)]
+            lin_b_got = [send2(lin_b_slab[j], j) for j in range(2)]
+            lin_own = [add2(lin_part[j], after(lin_got[j], lin_b_slab), j) for j in range(2)]
+            lin_z = [swap_z(v) for v in lin_own]
+            d_norm = after(d_norm, lin_own) + d_norm_term(3, ours, lin_own) + d_norm_got
+            lin_b_got = after(lin_b_got, d_norm)
             d_h = inv_rms * (d_norm - normed * jnp.mean(d_norm * normed, axis=-1, keepdims=True))
             grad_acc = grad_acc + d_h
-            lin_own = [add2(lin_part[j], after(lin_got[j], lin_b_slab), j) for j in range(2)]
-            lin_z = [swap_z(v) for v in lin_own]
-            lin_b_part = [add1(lin[1][j], after(lin_b_got[j], lin_own), j) for j in range(2)]
-            lin_b_slab = [slab2(lin_b_part[j], j) for j in range(2)]
-            lin_b_got = [send2(lin_b_slab[j], j) for j in range(2)]
             lin_b_own = [add2(lin_b_part[j], lin_b_got[j], j) for j in range(2)]
             lin_b_z = [swap_z(v) for v in lin_b_own]
             down_z0, down_z1, up_z0, up_z1, lin_z = after((down_z0, down_z1, up_z0, up_z1, lin_z), lin_b_own)

time: 1550 us -> 1430 us (0.923)
  waiting for transfers between devices: 650 us -> 518 us
    ppermute x25, waiting for transfers between devices: 300 us -> 219 us  [swap(): return lax.ppermute(value, 'fsdp', [(i, i ^ bit) for i in range(n_fsdp)])]
    ppermute x8, waiting for transfers between devices: 240 us -> 189 us  [swap_z(): return lax.ppermute(value, 'replica', [(0, 1), (1, 0)])]
  transfers between devices with their start and end apart: 36 -> 36, of which waited for: 18 -> 19; matrix products, arithmetic and copies ran while one was open for 47% -> 56% of each run, Pallas kernels for 0% -> 0%
where the time goes in v3:
time: 1430 us; the launch traced here: 1420 us
  matrix products  603 us (42%)
  waiting for transfers between devices  518 us (36%)
  local copies, waits for them, and re-layouts  131 us (9%)
  other arithmetic  131 us (9%)
  starting transfers between devices  26.5 us (2%)
  between operations  14.5 us (1%)
    dot_general x20, matrix products, dot(): lax.dot_general(a, b, (((da,), (db,)), ((), ())), preferred_element_type=...  603 us
    ppermute x25, waiting for transfers between devices, swap(): return lax.ppermute(value, 'fsdp', [(i, i ^ bit) for i in range(n_fsdp)])  219 us
    ppermute x8, waiting for transfers between devices, swap_z(): return lax.ppermute(value, 'replica', [(0, 1), (1, 0)])  189 us
    all_gather x1, waiting for transfers between devices, local_step(): lin_w = take_cols(lax.all_gather(lin_eo, 'fsdp', axis=0, tiled=True))  56.1 us
    all_gather x1, waiting for transfers between devices, local_step(): up_w = take_cols(lax.all_gather(up_eo, 'fsdp', axis=0, tiled=True))  53.6 us
    squeeze x16, local copies, waits for them, and re-layouts, pick(): return lax.dynamic_index_in_dim(arr, idx, axis, keepdims=False)  43.3 us
    add x8, other arithmetic, add1(): return pick(g, pos[first], 1 - first) + got  29 us
  transfers between devices with their start and end apart: 36, of which 19 were waited for; matrix products, arithmetic and copies ran while one was open for 56% of the time, Pallas kernels for 0%

profile of v3, /device:TPU:0, one launch (start us, length us, event | category | flops | bytes accessed | tf_op | source)
XLA Modules:
  0.0 1423.6 jit_solution(5790049946901618108)
XLA Ops:
  79.4 53.6 %all-gather.4.cloned.1.call-done = bf16[2048,5632]{1,0:T(8,128)(2,1)} async-done(((bf16[256,5632]{1,0:T(8,128)(2,1)}), bf16[2048,5632]{1,0:T(8,128)(2,1)}) %all-gather.4.cloned.1.call-update) | async-done | bytes 23068688 | tf_op jit(solution)/shard_map/all_gather | solution.py:96
  133.1 58.9 %fusion.11 = f32[4096,2816]{1,0:T(8,128)} fusion(bf16[2048,5632]{1,0:T(8,128)(2,1)} %all-gather.4.cloned.1.call-done, s32[]{:T(128)S(6)} %select_n.137, bf16[2048,2048]{1,0:T(8,128)(2,1)} %collective-permute-done, bf16[2048,2048]{1,0:T(8,128)(2,1)} %fusion.2), kind=kOutput, calls=%fused_computation.24 | convolution fusion | flops 47278194688 | bytes 74448896 | tf_op jit(solution)/shard_map/dot_general | solution.py:13
  192.0 56.1 %all-gather.6.cloned.1.call-done = bf16[2048,5632]{1,0:T(8,128)(2,1)} async-done(((bf16[256,5632]{1,0:T(8,128)(2,1)}), bf16[2048,5632]{1,0:T(8,128)(2,1)}) %all-gather.6.cloned.1.call-update) | async-done | bytes 23068688 | tf_op jit(solution)/shard_map/all_gather | solution.py:97
  248.1 63.9 %multiply_convert_fusion = (bf16[4096,2816]{1,0:T(8,128)(2,1)}, f32[4096,2816]{1,0:T(8,128)}) fusion(f32[4096,2816]{1,0:T(8,128)} %fusion.11, bf16[2048,5632]{1,0:T(8,128)(2,1)} %all-gather.6.cloned.1.call-done, s32[]{:T(128)S(6)} %select_n.137, bf16[2048,2048]{1,0:T(8,128)(2,1)} %collective-permute-done, bf16[2048,2048]{1,0:T(8,128)(2,1)} %fusion.2), kind=kOutput, calls=%fused_computation | convolution fusion | flops 47347400704 | bytes 143654912 | tf_op jit(solution)/shard_map/dot_general | solution.py:13
  312.0 34.0 %fusion.15 = f32[2816,1024]{1,0:T(8,128)} fusion(bf16[4096,2816]{1,0:T(8,128)(2,1)} %get-tuple-element.54, bf16[4096,2048]{1,0:T(8,128)(2,1)} %constant_dynamic-update-slice_fusion), kind=kOutput, calls=%fused_computation.28 | convolution fusion | flops 23622320128 | bytes 42991616 | tf_op jit(solution)/shard_map/dot_general | solution.py:13
  353.5 34.1 %fusion.13 = f32[2816,1024]{1,0:T(8,128)} fusion(bf16[4096,2816]{1,0:T(8,128)(2,1)} %get-tuple-element.54, bf16[4096,2048]{1,0:T(8,128)(2,1)} %constant_dynamic-update-slice_fusion), kind=kOutput, calls=%fused_computation.26 | convolution fusion | flops 23622320128 | bytes 42991616 | tf_op jit(solution)/shard_map/dot_general | solution.py:13
  405.5 41.5 %multiply_convert_fusion.2 = (bf16[4096,1408]{1,0:T(8,128)(2,1)}, bf16[4096,1408]{1,0:T(8,128)(2,1)}) fusion(f32[4096,2816]{1,0:T(8,128)} %fusion.11, f32[4096,2816]{1,0:T(8,128)} %get-tuple-element.57, bf16[4096,2048]{1,0:T(8,128)(2,1)} %constant_dynamic-update-slice_fusion, bf16[1408,2048]{1,0:T(8,128)(2,1)} %bitcast.130), kind=kOutput, calls=%fused_computation.2 | convolution fusion | flops 23697293312 | bytes 91750400 | tf_op jit(solution)/shard_map/dot_general | solution.py:13
  447.0 33.2 %fusion.57 = f32[2048,1408]{1,0:T(8,128)S(1)} fusion(bf16[4096,1408]{1,0:T(8,128)(2,1)} %get-tuple-element.80, bf16[2048,2048]{1,0:T(8,128)(2,1)} %collective-permute-done, bf16[2048,2048]{1,0:T(8,128)(2,1)} %fusion.2), kind=kOutput, calls=%fused_computation.132 | convolution fusion | flops 23655874560 | bytes 39845888 | tf_op jit(solution)/shard_map/dot_general | solution.py:13
  497.6 41.7 %multiply_convert_fusion.1 = (bf16[4096,1408]{1,0:T(8,128)(2,1)}, bf16[4096,1408]{1,0:T(8,128)(2,1)}) fusion(f32[4096,2816]{1,0:T(8,128)} %fusion.11, f32[4096,2816]{1,0:T(8,128)} %get-tuple-element.57, bf16[4096,2048]{1,0:T(8,128)(2,1)} %constant_dynamic-update-slice_fusion, bf16[1408,2048]{1,0:T(8,128)(2,1)} %bitcast.129), kind=kOutput, calls=%fused_computation.1 | convolution fusion | flops 23697293312 | bytes 91750400 | tf_op jit(solution)/shard_map/dot_general | solution.py:13
  539.3 33.4 %fusion.56 = f32[2048,1408]{1,0:T(8,128)S(1)} fusion(bf16[4096,1408]{1,0:T(8,128)(2,1)} %get-tuple-element.84, bf16[2048,2048]{1,0:T(8,128)(2,1)} %collective-permute-done, bf16[2048,2048]{1,0:T(8,128)(2,1)} %fusion.2), kind=kOutput, calls=%fused_computation.131 | convolution fusion | flops 23655874560 | bytes 39845888 | tf_op jit(solution)/shard_map/dot_general | solution.py:13
  604.8 21.0 %fusion.35 = f32[2048,640]{1,0:T(8,128)} fusion(bf16[4096,2048]{1,0:T(8,128)(2,1)} %pad_maximum_fusion, bf16[4096,1408]{1,0:T(8,128)(2,1)} %get-tuple-element.85), kind=kOutput, calls=%fused_computation.58 | convolution fusion | flops 10737418240 | bytes 27262976 | tf_op jit(solution)/shard_map/dot_general | solution.py:13
  630.9 21.0 %fusion.17 = f32[2048,768]{1,0:T(8,128)} fusion(bf16[4096,2048]{1,0:T(8,128)(2,1)} %pad_maximum_fusion, bf16[4096,1408]{1,0:T(8,128)(2,1)} %get-tuple-element.91), kind=kOutput, calls=%fused_computation.31 | convolution fusion | flops 12884901888 | bytes 29360128 | tf_op jit(solution)/shard_map/dot_general | solution.py:13
  694.0 59.9 %collective-permute-done.7 = f32[2,512,1408]{2,1,0:T(8,128)} collective-permute-done((f32[2,512,1408]{2,1,0:T(8,128)}, f32[2,512,1408]{2,1,0:T(8,128)}, u32[]{:S(2)}, u32[]{:S(2)}) %collective-permute-start.7) | collective-permute-done | bytes 5767200 | tf_op jit(solution)/shard_map/ppermute | solution.py:31
  800.3 27.2 %add_add_fusion.2 = f32[2048,2048]{1,0:T(8,128)} fusion(f32[2048,2048]{1,0:T(8,128)} %fusion.31, f32[2048,2048]{1,0:T(8,128)} %fusion.29, bf16[4096,1408]{1,0:T(8,128)(2,1)} %get-tuple-element.80, bf16[2048,5632]{1,0:T(8,128)(2,1)} %all-gather.4.cloned.1.call-done, s32[]{:T(128)S(6)} %select_n.137), kind=kOutput, calls=%fused_computation.21 | convolution fusion | flops 11819548672 | bytes 61865988 | tf_op jit(solution)/shard_map/dot_general | solution.py:13
  838.8 22.8 %convolution_add_fusion = f32[2048,2048]{1,0:T(8,128)} fusion(f32[2048,2048]{1,0:T(8,128)} %add_add_fusion.2, bf16[4096,1408]{1,0:T(8,128)(2,1)} %get-tuple-element.91, bf16[2048,5632]{1,0:T(8,128)(2,1)} %all-gather.6.cloned.1.call-done, s32[]{:T(128)S(6)} %add.248), kind=kOutput, calls=%fused_computation.30 | convolution fusion | flops 11815354368 | bytes 45088772 | tf_op jit(solution)/shard_map/dot_general | solution.py:13
  885.3 41.9 %collective-permute-done.12 = f32[512,1408]{1,0:T(8,128)S(1)} collective-permute-done((f32[512,1408]{1,0:T(8,128)}, f32[512,1408]{1,0:T(8,128)S(1)}, u32[]{:S(2)}, u32[]{:S(2)}) %collective-permute-start.12) | collective-permute-done | bytes 2883616 | tf_op jit(solution)/shard_map/ppermute | solution.py:31
  934.8 59.8 %collective-permute-done.14 = f32[2,512,768]{2,1,0:T(8,128)S(1)} collective-permute-done((f32[2,512,768]{2,1,0:T(8,128)S(1)}, f32[2,512,768]{2,1,0:T(8,128)S(1)}, u32[]{:S(2)}, u32[]{:S(2)}) %collective-permute-start.14) | collective-permute-done | bytes 3145760 | tf_op jit(solution)/shard_map/ppermute | solution.py:31
  1022.4 26.9 %add_add_fusion.1 = f32[2048,2048]{1,0:T(8,128)} fusion(f32[2048,2048]{1,0:T(8,128)} %fusion.25, f32[2048,2048]{1,0:T(8,128)} %fusion.23, bf16[4096,1408]{1,0:T(8,128)(2,1)} %get-tuple-element.85, bf16[2048,5632]{1,0:T(8,128)(2,1)} %all-gather.6.cloned.1.call-done, s32[]{:T(128)S(6)} %select_n.137), kind=kOutput, calls=%fused_computation.20 | convolution fusion | flops 11819548672 | bytes 61865988 | tf_op jit(solution)/shard_map/dot_general | solution.py:13
  1062.6 22.0 %collective-permute-done.20 = f32[512,768]{1,0:T(8,128)} collective-permute-done((f32[512,768]{1,0:T(8,128)}, f32[512,768]{1,0:T(8,128)}, u32[]{:S(2)}, u32[]{:S(2)}) %collective-permute-start.20) | collective-permute-done | bytes 1572896 | tf_op jit(solution)/shard_map/ppermute | solution.py:31
  1116.8 27.4 %fusion.3 = (f32[2048]{0:T(1024)S(1)}, f32[2048,2048]{1,0:T(8,128)}) fusion(bf16[1,2048,2048]{2,1,0:T(8,128)(2,1)} %param.5, f32[2048]{0:T(1024)S(1)} %copy-done.18, f32[2048,2048]{1,0:T(8,128)} %collective-permute-done.24, f32[2048,2048]{1,0:T(8,128)} %add_add_fusion.1, bf16[2048,5632]{1,0:T(8,128)(2,1)} %all-gather.6.cloned.1.call-done, s32[]{:T(128)S(6)} %add.248, ...), kind=kOutput, calls=%fused_computation.12 | convolution fusion | flops 11836323840 | bytes 70270976 | tf_op jit(solution)/shard_map/dot_general | solution.py:13
  1152.3 60.3 %collective-permute-done.11 = f32[512,1408]{1,0:T(8,128)} collective-permute-done((f32[512,1408]{1,0:T(8,128)}, f32[512,1408]{1,0:T(8,128)}, u32[]{:S(2)}, u32[]{:S(2)}) %collective-permute-start.11) | collective-permute-done | bytes 2883616 | tf_op jit(solution)/shard_map/ppermute | solution.py:34
  1214.1 60.3 %collective-permute-done.13 = f32[512,1408]{1,0:T(8,128)} collective-permute-done((f32[512,1408]{1,0:T(8,128)}, f32[512,1408]{1,0:T(8,128)}, u32[]{:S(2)}, u32[]{:S(2)}) %collective-permute-start.13) | collective-permute-done | bytes 2883616 | tf_op jit(solution)/shard_map/ppermute | solution.py:34
  1274.4 33.7 %collective-permute-done.21 = f32[512,768]{1,0:T(8,128)} collective-permute-done((f32[512,768]{1,0:T(8,128)}, f32[512,768]{1,0:T(8,128)}, u32[]{:S(2)}, u32[]{:S(2)}) %collective-permute-start.21) | collective-permute-done | bytes 1572896 | tf_op jit(solution)/shard_map/ppermute | solution.py:34
  1308.1 33.7 %collective-permute-done.19 = f32[512,768]{1,0:T(8,128)} collective-permute-done((f32[512,768]{1,0:T(8,128)S(1)}, f32[512,768]{1,0:T(8,128)}, u32[]{:S(2)}, u32[]{:S(2)}) %collective-permute-start.19) | collective-permute-done | bytes 1572896 | tf_op jit(solution)/shard_map/ppermute | solution.py:34
  (223 shorter events, 440.7 us)
Async XLA Ops:
  7.2 125.9 %all-gather.4.cloned.1.call-start = ((), (), s32[]{:S(2)}) async-start(), calls=%async_computation | async-start | bytes 25952256 | tf_op jit(solution)/shard_map/all_gather | solution.py:96
  17.6 230.6 %all-gather.6.cloned.1.call-start = ((), (), s32[]{:S(2)}) async-start(), calls=%async_computation.1 | async-start | bytes 25952256 | tf_op jit(solution)/shard_map/all_gather | solution.py:97
  25.9 368.4 %all-gather.8.cloned.1.call-start = ((), (), s32[]{:S(2)}) async-start(), calls=%async_computation.2 | async-start | bytes 25952256 | tf_op jit(solution)/shard_map/all_gather | solution.py:98
  352.1 134.0 %collective-permute-start.3 = (f32[2,704,1024]{2,1,0:T(8,128)}, f32[2,704,1024]{2,1,0:T(8,128)}, u32[]{:S(2)}, u32[]{:S(2)}) collective-permute-start(f32[2,704,1024]{2,1,0:T(8,128)} %dynamic-slice_bitcast_fusion.3), channel_id=1, source_target_pairs={{0,2},{1,3},{2,0},{3,1},{4,6},{5,7},{6,4},{7,5},{8,10},{9,11},{10,... | collective-permute-start | bytes 17301512 | tf_op jit(solution)/shard_map/ppermute | solution.py:31
  393.8 184.9 %collective-permute-start.5 = (f32[2,704,1024]{2,1,0:T(8,128)}, f32[2,704,1024]{2,1,0:T(8,128)}, u32[]{:S(2)}, u32[]{:S(2)}) collective-permute-start(f32[2,704,1024]{2,1,0:T(8,128)} %dynamic-slice_bitcast_fusion.2), channel_id=1, source_target_pairs={{0,4},{1,5},{2,6},{3,7},{4,0},{5,1},{6,2},{7,3},{8,12},{9,13},{10,... | collective-permute-start | bytes 17301512 | tf_op jit(solution)/shard_map/ppermute | solution.py:31
  483.4 187.5 %collective-permute-start.2 = (f32[2,512,1408]{2,1,0:T(8,128)}, f32[2,512,1408]{2,1,0:T(8,128)}, u32[]{:S(2)}, u32[]{:S(2)}) collective-permute-start(f32[2,512,1408]{2,1,0:T(8,128)} %dynamic-slice_bitcast_fusion.1), channel_id=1, source_target_pairs={{0,2},{1,3},{2,0},{3,1},{4,6},{5,7},{6,4},{7,5},{8,10},{9,11},{10,... | collective-permute-start | bytes 17301512 | tf_op jit(solution)/shard_map/ppermute | solution.py:31
  496.1 130.8 %collective-permute-start.4 = (f32[704,1024]{1,0:T(8,128)}, f32[704,1024]{1,0:T(8,128)}, u32[]{:S(2)}, u32[]{:S(2)}) collective-permute-start(f32[704,1024]{1,0:T(8,128)} %dynamic-slice_bitcast_fusion.9), channel_id=1, source_target_pairs={{0,4},{1,5},{2,6},{3,7},{4,0},{5,1},{6,2},{7,3},{8,12},{9,13},{10,... | collective-permute-start | bytes 8650760 | tf_op jit(solution)/shard_map/ppermute | solution.py:31
  626.4 127.5 %collective-permute-start.7 = (f32[2,512,1408]{2,1,0:T(8,128)}, f32[2,512,1408]{2,1,0:T(8,128)}, u32[]{:S(2)}, u32[]{:S(2)}) collective-permute-start(f32[2,512,1408]{2,1,0:T(8,128)} %dynamic-slice_bitcast_fusion), channel_id=1, source_target_pairs={{0,4},{1,5},{2,6},{3,7},{4,0},{5,1},{6,2},{7,3},{8,12},{9,13},{10,... | collective-permute-start | bytes 17301512 | tf_op jit(solution)/shard_map/ppermute | solution.py:31
  677.7 149.7 %collective-permute-start.6 = (f32[512,1408]{1,0:T(8,128)}, f32[512,1408]{1,0:T(8,128)}, u32[]{:S(2)}, u32[]{:S(2)}) collective-permute-start(f32[512,1408]{1,0:T(8,128)} %dynamic-slice_bitcast_fusion.7), channel_id=1, source_target_pairs={{0,4},{1,5},{2,6},{3,7},{4,0},{5,1},{6,2},{7,3},{8,12},{9,13},{10,... | collective-permute-start | bytes 8650760 | tf_op jit(solution)/shard_map/ppermute | solution.py:31
  861.6 254.6 %collective-permute-start.24 = (f32[2048,2048]{1,0:T(8,128)}, f32[2048,2048]{1,0:T(8,128)}, u32[]{:S(2)}, u32[]{:S(2)}) collective-permute-start(f32[2048,2048]{1,0:T(8,128)} %convolution_add_fusion), channel_id=1, source_target_pairs={{0,1},{1,0},{2,3},{3,2},{4,5},{5,4},{6,7},{7,6},{8,9},{9,8},{10,11... | collective-permute-start | bytes 50331656 | tf_op jit(solution)/shard_map/ppermute | solution.py:31
  861.6 65.6 %collective-permute-start.12 = (f32[512,1408]{1,0:T(8,128)}, f32[512,1408]{1,0:T(8,128)S(1)}, u32[]{:S(2)}, u32[]{:S(2)}) collective-permute-start(f32[512,1408]{1,0:T(8,128)} %dynamic-slice_bitcast_fusion.6), channel_id=1, source_target_pairs={{0,2},{1,3},{2,0},{3,1},{4,6},{5,7},{6,4},{7,5},{8,10},{9,11},{10,... | collective-permute-start | bytes 8650760 | tf_op jit(solution)/shard_map/ppermute | solution.py:31
  863.0 71.2 %collective-permute-start.17 = (f32[2,512,768]{2,1,0:T(8,128)}, f32[2,512,768]{2,1,0:T(8,128)S(1)}, u32[]{:S(2)}, u32[]{:S(2)}) collective-permute-start(f32[2,512,768]{2,1,0:T(8,128)} %dynamic-slice_bitcast_fusion.4), channel_id=1, source_target_pairs={{0,4},{1,5},{2,6},{3,7},{4,0},{5,1},{6,2},{7,3},{8,12},{9,13},{10,... | collective-permute-start | bytes 9437192 | tf_op jit(solution)/shard_map/ppermute | solution.py:31
  863.5 131.1 %collective-permute-start.14 = (f32[2,512,768]{2,1,0:T(8,128)S(1)}, f32[2,512,768]{2,1,0:T(8,128)S(1)}, u32[]{:S(2)}, u32[]{:S(2)}) collective-permute-start(f32[2,512,768]{2,1,0:T(8,128)S(1)} %copy-done.16), channel_id=1, source_target_pairs={{0,2},{1,3},{2,0},{3,1},{4,6},{5,7},{6,4},{7,5},{8,10},{9,11},{10,... | collective-permute-start | bytes 9437192 | tf_op jit(solution)/shard_map/ppermute | solution.py:31
  864.1 227.3 %collective-permute-start.10 = (f32[704,1024]{1,0:T(8,128)}, f32[704,1024]{1,0:T(8,128)}, u32[]{:S(2)}, u32[]{:S(2)}) collective-permute-start(f32[704,1024]{1,0:T(8,128)} %bitcast_add_fusion.7), channel_id=1, source_target_pairs={{0,8},{8,0},{1,9},{9,1},{2,10},{10,2},{3,11},{11,3},{4,12},{12,4},... | collective-permute-start | bytes 8650760 | tf_op jit(solution)/shard_map/ppermute | solution.py:34
  927.2 122.1 %collective-permute-start.18 = (f32[2,512,640]{2,1,0:T(8,128)}, f32[2,512,640]{2,1,0:T(8,128)}, u32[]{:S(2)}, u32[]{:S(2)}) collective-permute-start(f32[2,512,640]{2,1,0:T(8,128)} %dynamic-slice_bitcast_fusion.10), channel_id=1, source_target_pairs={{0,4},{1,5},{2,6},{3,7},{4,0},{5,1},{6,2},{7,3},{8,12},{9,13},{10,... | collective-permute-start | bytes 7864328 | tf_op jit(solution)/shard_map/ppermute | solution.py:31
  934.1 116.7 %collective-permute-start.16 = (f32[2,512,640]{2,1,0:T(8,128)}, f32[2,512,640]{2,1,0:T(8,128)}, u32[]{:S(2)}, u32[]{:S(2)}) collective-permute-start(f32[2,512,640]{2,1,0:T(8,128)} %dynamic-slice_bitcast_fusion.11), channel_id=1, source_target_pairs={{0,2},{1,3},{2,0},{3,1},{4,6},{5,7},{6,4},{7,5},{8,10},{9,11},{10,... | collective-permute-start | bytes 7864328 | tf_op jit(solution)/shard_map/ppermute | solution.py:31
  1001.8 82.8 %collective-permute-start.20 = (f32[512,768]{1,0:T(8,128)}, f32[512,768]{1,0:T(8,128)}, u32[]{:S(2)}, u32[]{:S(2)}) collective-permute-start(f32[512,768]{1,0:T(8,128)} %dynamic-slice_bitcast_fusion.12), channel_id=1, source_target_pairs={{0,2},{1,3},{2,0},{3,1},{4,6},{5,7},{6,4},{7,5},{8,10},{9,11},{10,... | collective-permute-start | bytes 4718600 | tf_op jit(solution)/shard_map/ppermute | solution.py:31
  1085.1 65.7 %collective-permute-start.9 = (f32[704,1024]{1,0:T(8,128)}, f32[704,1024]{1,0:T(8,128)}, u32[]{:S(2)}, u32[]{:S(2)}) collective-permute-start(f32[704,1024]{1,0:T(8,128)} %bitcast_add_fusion.9), channel_id=1, source_target_pairs={{0,8},{8,0},{1,9},{9,1},{2,10},{10,2},{3,11},{11,3},{4,12},{12,4},... | collective-permute-start | bytes 8650760 | tf_op jit(solution)/shard_map/ppermute | solution.py:34
  1091.5 121.1 %collective-permute-start.11 = (f32[512,1408]{1,0:T(8,128)}, f32[512,1408]{1,0:T(8,128)}, u32[]{:S(2)}, u32[]{:S(2)}) collective-permute-start(f32[512,1408]{1,0:T(8,128)} %bitcast_add_fusion.8), channel_id=1, source_target_pairs={{0,8},{8,0},{1,9},{9,1},{2,10},{10,2},{3,11},{11,3},{4,12},{12,4},... | collective-permute-start | bytes 8650760 | tf_op jit(solution)/shard_map/ppermute | solution.py:34
  1112.2 162.2 %collective-permute-start.13 = (f32[512,1408]{1,0:T(8,128)}, f32[512,1408]{1,0:T(8,128)}, u32[]{:S(2)}, u32[]{:S(2)}) collective-permute-start(f32[512,1408]{1,0:T(8,128)} %bitcast_add_fusion.6), channel_id=1, source_target_pairs={{0,8},{8,0},{1,9},{9,1},{2,10},{10,2},{3,11},{11,3},{4,12},{12,4},... | collective-permute-start | bytes 8650760 | tf_op jit(solution)/shard_map/ppermute | solution.py:34
  1114.8 193.3 %collective-permute-start.21 = (f32[512,768]{1,0:T(8,128)}, f32[512,768]{1,0:T(8,128)}, u32[]{:S(2)}, u32[]{:S(2)}) collective-permute-start(f32[512,768]{1,0:T(8,128)} %bitcast_add_fusion.12), channel_id=1, source_target_pairs={{0,8},{8,0},{1,9},{9,1},{2,10},{10,2},{3,11},{11,3},{4,12},{12,4},... | collective-permute-start | bytes 4718600 | tf_op jit(solution)/shard_map/ppermute | solution.py:34
  1116.2 225.6 %collective-permute-start.19 = (f32[512,768]{1,0:T(8,128)S(1)}, f32[512,768]{1,0:T(8,128)}, u32[]{:S(2)}, u32[]{:S(2)}) collective-permute-start(f32[512,768]{1,0:T(8,128)S(1)} %bitcast_add_fusion.13), channel_id=1, source_target_pairs={{0,8},{8,0},{1,9},{9,1},{2,10},{10,2},{3,11},{11,3},{4,12},{12,4},... | collective-permute-start | bytes 4718600 | tf_op jit(solution)/shard_map/ppermute | solution.py:34
  1150.8 247.5 %collective-permute-start.29 = (f32[512,640]{1,0:T(8,128)}, f32[512,640]{1,0:T(8,128)}, u32[]{:S(2)}, u32[]{:S(2)}) collective-permute-start(f32[512,640]{1,0:T(8,128)} %bitcast_add_fusion.14), channel_id=1, source_target_pairs={{0,8},{8,0},{1,9},{9,1},{2,10},{10,2},{3,11},{11,3},{4,12},{12,4},... | collective-permute-start | bytes 3932168 | tf_op jit(solution)/shard_map/ppermute | solution.py:34
  1212.6 185.7 %collective-permute-start.28 = (f32[512,640]{1,0:T(8,128)}, f32[512,640]{1,0:T(8,128)}, u32[]{:S(2)}, u32[]{:S(2)}) collective-permute-start(f32[512,640]{1,0:T(8,128)} %bitcast_add_fusion.15), channel_id=1, source_target_pairs={{0,8},{8,0},{1,9},{9,1},{2,10},{10,2},{3,11},{11,3},{4,12},{12,4},... | collective-permute-start | bytes 3932168 | tf_op jit(solution)/shard_map/ppermute | solution.py:34
  (47 other events, 1345.5 us)
Sparse Core Ops, SparseCore 0:
  17.7 115.3 all-gather.3
  135.5 112.5 all-gather.5
  250.0 116.0 all-gather.7
